TPU v7x, 256 devices: a whole 4x4x8 slice. The times are simulated.
256 devices in a mesh: tm: 32 (over y_hi, z, core), asset: 8 (over x, y_lo).
Axes of the slice: x: 4, y: 4 (y_hi: 2, y_lo: 2; y = y_hi * 2 + y_lo), z: 8, core: 2. Of those that a mesh axis runs over, the one named last changes fastest.
Arguments:
- returns: bfloat16 [128, 8192], P('tm', 'asset'), as said below
- signal: bfloat16 [128, 8192], P('tm', 'asset'), may hold values from -6 to 6
- earlier: bfloat16 [59, 8192], P(None, 'asset'), as said below
Outputs:
- filtered: float32 [128, 8192], P('tm', 'asset')
Inputs may be any that keep to these rules, and one draw needn't show every extreme that they name: Each equity has its own scale of returns, the same in returns and earlier. `earlier`: drawn by the same law as returns, with the same scale for each equity.
All inputs are finite; a program needn't handle non-finite values.
Results may differ from a plain program's by a relative error of at most 0.0032.
Values may be sent and summed in bfloat16 or wider, within the bound.
A program may use at most 64 MiB of HBM per device.

v0:
```python
import jax
import jax.numpy as jnp
from jax import lax
from jax.sharding import PartitionSpec as P

WIN = 60
HIST = 59


var_floor = 0.05
shrink_level = 0.1


def passed_along(value, axis, by):
    peers = lax.axis_size(axis)
    pairs = [(i, i + by) for i in range(peers) if 0 <= i + by < peers]
    return lax.ppermute(value, axis, pairs)


def copy_for_each(value, axis):
    copies = jnp.broadcast_to(value, (lax.axis_size(axis), *value.shape))
    return lax.all_to_all(copies, axis, split_axis=0, concat_axis=0, tiled=True)


def laid_out(pieces, dim):
    pieces = jnp.moveaxis(pieces, 0, dim)
    shape = pieces.shape
    return pieces.reshape(*shape[:dim], shape[dim] * shape[dim + 1], *shape[dim + 2 :])


def gathered_copies(value, axis, dim):
    pieces = copy_for_each(value, axis)
    return laid_out(pieces, dim)


def in_one_piece(arrays, axis, dim, along):
    both = jnp.concatenate(arrays, axis=along)
    result, at, outs = (gathered_copies(both, axis, dim), 0, [])
    for a in arrays:
        outs.append(lax.slice_in_dim(result, at, at + a.shape[along], axis=along))
        at += a.shape[along]
    return tuple(outs)


def moments(window):
    values = window.astype(jnp.float32)
    center = jnp.mean(values, axis=0)
    spread = jnp.mean(values * values, axis=0) - center * center
    return (center, jnp.sqrt(jnp.maximum(spread, var_floor)))


def contribution(ext_rows, ext_cols, signal_cols):

    def one_day(day_index):
        window_rows = lax.dynamic_slice_in_dim(ext_rows, day_index, WIN, 0)
        window_cols = lax.dynamic_slice_in_dim(ext_cols, day_index, WIN, 0)
        mean_rows, scale_rows = moments(window_rows)
        mean_cols, scale_cols = moments(window_cols)
        gram_tile = lax.dot_general(
            window_rows, window_cols, (((0,), (0,)), ((), ())), preferred_element_type=jnp.float32
        )
        correlation = (gram_tile / WIN - mean_rows[:, None] * mean_cols[None, :]) / (
            scale_rows[:, None] * scale_cols[None, :]
        )
        shrunk = (
            jnp.sign(correlation) * jnp.maximum(jnp.abs(correlation) - shrink_level, 0.0)
        ).astype(jnp.bfloat16)
        day_signal = lax.dynamic_index_in_dim(signal_cols, day_index, 0, keepdims=False)
        return jnp.dot(shrunk, day_signal, preferred_element_type=jnp.float32)

    return lax.map(one_day, jnp.arange(signal_cols.shape[0], dtype=jnp.int32))


def history(block_rows, earlier_rows):
    day_dev = block_rows.shape[0]
    position = lax.axis_index("tm")
    span = HIST + day_dev
    blocks_needed = -(-HIST // day_dev)
    stacked = block_rows
    for level in range(blocks_needed.bit_length()):
        moved = passed_along(stacked, "tm", 1 << level)
        stacked = jnp.concatenate([moved, stacked], 0)
    tail_rows = stacked[stacked.shape[0] - span :]
    padded = jnp.concatenate(
        [earlier_rows, jnp.zeros((span, earlier_rows.shape[1]), earlier_rows.dtype)], 0
    )
    filler = lax.dynamic_slice_in_dim(padded, position * day_dev, span, 0)
    offsets = position * day_dev - HIST + jnp.arange(span, dtype=jnp.int32)
    return jnp.where((offsets < 0)[:, None], filler, tail_rows)


def per_device(returns, signal, earlier):
    extended = history(returns, earlier)
    pieces = in_one_piece((extended, signal), "asset", 1, 0)
    return contribution(extended, pieces[0], pieces[1])


def solution(mesh):
    in_specs = (P("tm", "asset"), P("tm", "asset"), P(None, "asset"))
    out_specs = P("tm", "asset")
    return jax.shard_map(
        per_device, mesh=mesh, in_specs=in_specs, out_specs=out_specs, check_vma=False
    )
```

profile of v0, /device:TPU:16, one launch (start us, length us, event | category | flops | bytes accessed | tf_op | source)
XLA Modules:
  0.0 163.7 jit_solution(11074274738785415078)
XLA Ops:
  0.0 1.9 %collective-permute-start = (bf16[4,1024]{1,0:T(4,128)(2,1)}, bf16[4,1024]{1,0:T(4,128)(2,1)S(1)}, u32[]{:S(2)}, u32[]{:S(2)}) collective-permute-start(bf16[4,1024]{1,0:T(4,128)(2,1)} %param.5), channel_id=1, source_target_pairs={{0,8},{8,16},{16,24},{24,32},{32,40},{40,48},{48,56},{56,64},{64,7... | collective-permute-start | bytes 24584 | tf_op jit(solution)/shard_map/ppermute | solution.py:17
  1.9 6.9 %collective-permute-done = bf16[4,1024]{1,0:T(4,128)(2,1)S(1)} collective-permute-done((bf16[4,1024]{1,0:T(4,128)(2,1)}, bf16[4,1024]{1,0:T(4,128)(2,1)S(1)}, u32[]{:S(2)}, u32[]{:S(2)}) %collective-permute-start) | collective-permute-done | bytes 8224 | tf_op jit(solution)/shard_map/ppermute | solution.py:17
  8.8 0.7 pad_maximum_fusion.3
  9.5 1.9 %collective-permute-start.1 = (bf16[8,1024]{1,0:T(8,128)(2,1)S(1)}, bf16[8,1024]{1,0:T(8,128)(2,1)S(1)}, u32[]{:S(2)}, u32[]{:S(2)}) collective-permute-start(bf16[8,1024]{1,0:T(8,128)(2,1)S(1)} %pad_maximum_fusion.3), channel_id=1, source_target_pairs={{0,16},{8,24},{16,32},{24,40},{32,48},{40,56},{48,64},{56,72},{64,... | collective-permute-start | bytes 49160 | tf_op jit(solution)/shard_map/ppermute | solution.py:17
  11.4 7.3 %collective-permute-done.1 = bf16[8,1024]{1,0:T(8,128)(2,1)S(1)} collective-permute-done((bf16[8,1024]{1,0:T(8,128)(2,1)S(1)}, bf16[8,1024]{1,0:T(8,128)(2,1)S(1)}, u32[]{:S(2)}, u32[]{:S(2)}) %collective-permute-start.1) | collective-permute-done | bytes 16416 | tf_op jit(solution)/shard_map/ppermute | solution.py:17
  18.7 0.7 pad_maximum_fusion.2
  19.5 1.9 %collective-permute-start.2 = (bf16[16,1024]{1,0:T(8,128)(2,1)S(1)}, bf16[16,1024]{1,0:T(8,128)(2,1)S(1)}, u32[]{:S(2)}, u32[]{:S(2)}) collective-permute-start(bf16[16,1024]{1,0:T(8,128)(2,1)S(1)} %pad_maximum_fusion.2), channel_id=1, source_target_pairs={{0,32},{8,40},{16,48},{24,56},{32,64},{40,72},{48,80},{56,88},{64,... | collective-permute-start | bytes 98312 | tf_op jit(solution)/shard_map/ppermute | solution.py:17
  21.4 8.4 %collective-permute-done.2 = bf16[16,1024]{1,0:T(8,128)(2,1)S(1)} collective-permute-done((bf16[16,1024]{1,0:T(8,128)(2,1)S(1)}, bf16[16,1024]{1,0:T(8,128)(2,1)S(1)}, u32[]{:S(2)}, u32[]{:S(2)}) %collective-permute-start.2) | collective-permute-done | bytes 32800 | tf_op jit(solution)/shard_map/ppermute | solution.py:17
  29.8 0.7 pad_maximum_fusion.1
  30.5 1.9 %collective-permute-start.3 = (bf16[32,1024]{1,0:T(8,128)(2,1)S(1)}, bf16[32,1024]{1,0:T(8,128)(2,1)S(1)}, u32[]{:S(2)}, u32[]{:S(2)}) collective-permute-start(bf16[32,1024]{1,0:T(8,128)(2,1)S(1)} %pad_maximum_fusion.1), channel_id=1, source_target_pairs={{0,64},{8,72},{16,80},{24,88},{32,96},{40,104},{48,112},{56,120},{... | collective-permute-start | bytes 196616 | tf_op jit(solution)/shard_map/ppermute | solution.py:17
  32.4 11.6 %collective-permute-done.3 = bf16[32,1024]{1,0:T(8,128)(2,1)S(1)} collective-permute-done((bf16[32,1024]{1,0:T(8,128)(2,1)S(1)}, bf16[32,1024]{1,0:T(8,128)(2,1)S(1)}, u32[]{:S(2)}, u32[]{:S(2)}) %collective-permute-start.3) | collective-permute-done | bytes 65568 | tf_op jit(solution)/shard_map/ppermute | solution.py:17
  44.0 0.7 concatenate.25
  44.7 0.8 fusion.16
  45.6 0.7 pad_maximum_fusion
  46.3 1.2 broadcast_in_dim.29
  47.4 5.3 %all-to-all-start = ((bf16[8,67,1024]{2,1,0:T(8,128)(2,1)}), bf16[8,67,1024]{2,1,0:T(8,128)(2,1)S(1)}, u32[]{:S(2)}, u32[]{:S(2)}) async-start(bf16[8,67,1024]{2,1,0:T(8,128)(2,1)} %broadcast_in_dim.29), calls=%async_computation | async-start | bytes 2359296 | tf_op jit(solution)/shard_map/all_to_all | solution.py:22
  52.7 12.3 %all-to-all-done = bf16[8,67,1024]{2,1,0:T(8,128)(2,1)S(1)} async-done(((bf16[8,67,1024]{2,1,0:T(8,128)(2,1)}), bf16[8,67,1024]{2,1,0:T(8,128)(2,1)S(1)}, u32[]{:S(2)}, u32[]{:S(2)}) %all-to-all-start) | async-done | bytes 1097760 | tf_op jit(solution)/shard_map/all_to_all | solution.py:22
  65.0 0.1 slice.21
  65.1 0.6 copy.4
  65.7 0.1 pad.12
  65.8 0.6 copy.5
  66.4 96.7 %while.12 = (s32[]{:T(128)}, f32[4,1024]{1,0:T(4,128)S(1)}, s32[4]{0:T(128)S(1)}, bf16[63,1024]{1,0:T(8,128)(2,1)S(1)}, bf16[63,8192]{1,0:T(8,128)(2,1)S(1)}, /*...) while((s32[]{:T(128)}, f32[4,1024]{1,0:T(4,128)S(1)}, s32[4]{0:T(128)S(1)}, ...), condition=%wide.region_5.6_spmd, body=%wide.region_0.5_spmd.sunk | while | flops 1117924352 | bytes 2627264 | solution.py:71
  66.4 0.6 dynamic_slice.58
  69.8 0.1 convert_reduce_fusion.5
  69.9 0.5 convert_reduce_fusion.4
  70.4 20.1 %fusion.24 = f32[1,1024]{1,0:T(1,128)S(1)} fusion(f32[8192]{0:T(1024)S(1)} %get-tuple-element.150, f32[1024]{0:T(1024)S(1)} %get-tuple-element.153, f32[8192]{0:T(1024)S(1)} %get-tuple-element.154, f32[1024]{0:T(1024)S(1)} %get-tuple-element.155, bf16[63,8192]{1,0:T(8,128)(2,1)S(1)} %get-tuple-element.180, s32[]{:T(128)S(6)} %select_n.26, ...), kind=kOutput, calls=%fused_computation.1.clone.1 | convolution fusion | flops 1115684864 | bytes 1291776 | tf_op jit(solution)/shard_map/while/body/eval_jaxpr/dot_general | solution.py:69
  90.5 0.1 dynamic_update_slice.8
  90.6 0.6 dynamic_slice.58
  94.0 0.1 convert_reduce_fusion.5
  94.1 0.5 convert_reduce_fusion.4
  94.7 20.0 %fusion.24 = f32[1,1024]{1,0:T(1,128)S(1)} fusion(f32[8192]{0:T(1024)S(1)} %get-tuple-element.150, f32[1024]{0:T(1024)S(1)} %get-tuple-element.153, f32[8192]{0:T(1024)S(1)} %get-tuple-element.154, f32[1024]{0:T(1024)S(1)} %get-tuple-element.155, bf16[63,8192]{1,0:T(8,128)(2,1)S(1)} %get-tuple-element.180, s32[]{:T(128)S(6)} %select_n.26, ...), kind=kOutput, calls=%fused_computation.1.clone.1 | convolution fusion | flops 1115684864 | bytes 1291776 | tf_op jit(solution)/shard_map/while/body/eval_jaxpr/dot_general | solution.py:69
  114.7 0.1 dynamic_update_slice.8
  114.8 0.6 dynamic_slice.58
  118.2 0.1 convert_reduce_fusion.5
  118.3 0.5 convert_reduce_fusion.4
  118.8 20.0 %fusion.24 = f32[1,1024]{1,0:T(1,128)S(1)} fusion(f32[8192]{0:T(1024)S(1)} %get-tuple-element.150, f32[1024]{0:T(1024)S(1)} %get-tuple-element.153, f32[8192]{0:T(1024)S(1)} %get-tuple-element.154, f32[1024]{0:T(1024)S(1)} %get-tuple-element.155, bf16[63,8192]{1,0:T(8,128)(2,1)S(1)} %get-tuple-element.180, s32[]{:T(128)S(6)} %select_n.26, ...), kind=kOutput, calls=%fused_computation.1.clone.1 | convolution fusion | flops 1115684864 | bytes 1291776 | tf_op jit(solution)/shard_map/while/body/eval_jaxpr/dot_general | solution.py:69
  138.9 0.1 dynamic_update_slice.8
  138.9 0.6 dynamic_slice.58
  142.3 0.1 convert_reduce_fusion.5
  142.4 0.5 convert_reduce_fusion.4
  143.0 20.0 %fusion.24 = f32[1,1024]{1,0:T(1,128)S(1)} fusion(f32[8192]{0:T(1024)S(1)} %get-tuple-element.150, f32[1024]{0:T(1024)S(1)} %get-tuple-element.153, f32[8192]{0:T(1024)S(1)} %get-tuple-element.154, f32[1024]{0:T(1024)S(1)} %get-tuple-element.155, bf16[63,8192]{1,0:T(8,128)(2,1)S(1)} %get-tuple-element.180, s32[]{:T(128)S(6)} %select_n.26, ...), kind=kOutput, calls=%fused_computation.1.clone.1 | convolution fusion | flops 1115684864 | bytes 1291776 | tf_op jit(solution)/shard_map/while/body/eval_jaxpr/dot_general | solution.py:69
  163.0 0.1 dynamic_update_slice.8
  163.1 0.0 copy-start
  163.1 0.6 copy-done
  (12 shorter events, 0.2 us)
Async XLA Ops:
  0.0 8.8 %collective-permute-start = (bf16[4,1024]{1,0:T(4,128)(2,1)}, bf16[4,1024]{1,0:T(4,128)(2,1)S(1)}, u32[]{:S(2)}, u32[]{:S(2)}) collective-permute-start(bf16[4,1024]{1,0:T(4,128)(2,1)} %param.5), channel_id=1, source_target_pairs={{0,8},{8,16},{16,24},{24,32},{32,40},{40,48},{48,56},{56,64},{64,7... | collective-permute-start | bytes 24584 | tf_op jit(solution)/shard_map/ppermute | solution.py:17
  9.5 9.2 %collective-permute-start.1 = (bf16[8,1024]{1,0:T(8,128)(2,1)S(1)}, bf16[8,1024]{1,0:T(8,128)(2,1)S(1)}, u32[]{:S(2)}, u32[]{:S(2)}) collective-permute-start(bf16[8,1024]{1,0:T(8,128)(2,1)S(1)} %pad_maximum_fusion.3), channel_id=1, source_target_pairs={{0,16},{8,24},{16,32},{24,40},{32,48},{40,56},{48,64},{56,72},{64,... | collective-permute-start | bytes 49160 | tf_op jit(solution)/shard_map/ppermute | solution.py:17
  19.5 10.3 %collective-permute-start.2 = (bf16[16,1024]{1,0:T(8,128)(2,1)S(1)}, bf16[16,1024]{1,0:T(8,128)(2,1)S(1)}, u32[]{:S(2)}, u32[]{:S(2)}) collective-permute-start(bf16[16,1024]{1,0:T(8,128)(2,1)S(1)} %pad_maximum_fusion.2), channel_id=1, source_target_pairs={{0,32},{8,40},{16,48},{24,56},{32,64},{40,72},{48,80},{56,88},{64,... | collective-permute-start | bytes 98312 | tf_op jit(solution)/shard_map/ppermute | solution.py:17
  30.5 13.5 %collective-permute-start.3 = (bf16[32,1024]{1,0:T(8,128)(2,1)S(1)}, bf16[32,1024]{1,0:T(8,128)(2,1)S(1)}, u32[]{:S(2)}, u32[]{:S(2)}) collective-permute-start(bf16[32,1024]{1,0:T(8,128)(2,1)S(1)} %pad_maximum_fusion.1), channel_id=1, source_target_pairs={{0,64},{8,72},{16,80},{24,88},{32,96},{40,104},{48,112},{56,120},{... | collective-permute-start | bytes 196616 | tf_op jit(solution)/shard_map/ppermute | solution.py:17
  47.4 17.5 %all-to-all-start = ((bf16[8,67,1024]{2,1,0:T(8,128)(2,1)}), bf16[8,67,1024]{2,1,0:T(8,128)(2,1)S(1)}, u32[]{:S(2)}, u32[]{:S(2)}) async-start(bf16[8,67,1024]{2,1,0:T(8,128)(2,1)} %broadcast_in_dim.29), calls=%async_computation | async-start | bytes 2359296 | tf_op jit(solution)/shard_map/all_to_all | solution.py:22
  163.1 0.6 copy-start
where the time goes:
time: 165 us; the launch traced here: 164 us
  matrix products  80.2 us (49%)
  waiting for transfers between devices  46.4 us (28%)
  starting transfers between devices  12.9 us (8%)
  loops' own time  11.4 us (7%)
  local copies, waits for them, and re-layouts  6.41 us (4%)
  other arithmetic  6.28 us (4%)
    dot_general x4, matrix products, one_day(): return jnp.dot(shrunk, day_signal, preferred_element_type=jnp.float32)  80.2 us
    ppermute x4, waiting for transfers between devices, passed_along(): return lax.ppermute(value, axis, pairs)  34.1 us
    all_to_all x1, waiting for transfers between devices, copy_for_each(): return lax.all_to_all(copies, axis, split_axis=0, concat_axis=0, tiled=True)  12.3 us
    another operation x1, loops' own time, contribution(): return lax.map(one_day, jnp.arange(signal_cols.shape[0], dtype=jnp.int32))  11.4 us
    ppermute x4, starting transfers between devices, passed_along(): return lax.ppermute(value, axis, pairs)  7.67 us
    all_to_all x1, starting transfers between devices, copy_for_each(): return lax.all_to_all(copies, axis, split_axis=0, concat_axis=0, tiled=True)  5.26 us
  transfers between devices with their start and end apart: 5, of which 5 were waited for; matrix products, arithmetic and copies ran while one was open for 0% of the time, Pallas kernels for 0%

commit v1 on v0

v1 whole, which is shorter than its diff:
```python
import jax
import jax.numpy as jnp
from jax import lax
from jax.experimental import pallas as pl
from jax.experimental.pallas import tpu as pltpu
from jax.sharding import PartitionSpec as P

WIN = 60
HIST = 59
DEPTH = 64
TILE = 256
STRIP = 128
LAG = 4

var_floor = 0.05
shrink_level = 0.1


def passed_along(value, axis, by):
    peers = lax.axis_size(axis)
    pairs = [(i, i + by) for i in range(peers) if 0 <= i + by < peers]
    return lax.ppermute(value, axis, pairs)


def history(block_rows, earlier_rows):
    day_dev = block_rows.shape[0]
    position = lax.axis_index("tm")
    span = HIST + day_dev
    blocks_needed = -(-HIST // day_dev)
    stacked = block_rows
    for level in range(blocks_needed.bit_length()):
        moved = passed_along(stacked, "tm", 1 << level)
        stacked = jnp.concatenate([moved, stacked], 0)
    tail_rows = stacked[stacked.shape[0] - span :]
    padded = jnp.concatenate(
        [earlier_rows, jnp.zeros((span, earlier_rows.shape[1]), earlier_rows.dtype)], 0
    )
    filler = lax.dynamic_slice_in_dim(padded, position * day_dev, span, 0)
    offsets = position * day_dev - HIST + jnp.arange(span, dtype=jnp.int32)
    return jnp.where((offsets < 0)[:, None], filler, tail_rows)


def totals(x):
    middle = x[8:16]
    middle_sq = middle * middle
    for at in range(16, DEPTH - 8, 8):
        part = x[at : at + 8]
        middle = middle + part
        middle_sq = middle_sq + part * part
    return middle, middle_sq


def day_edges(x, day):
    row = lax.broadcasted_iota(jnp.int32, (8, x.shape[1]), 0)
    first = jnp.where(row >= day, x[:8], 0.0)
    last = jnp.where(row <= day + (WIN - 1 - (DEPTH - 8)), x[DEPTH - 8 :], 0.0)
    return first, last


def day_moments(x, middle, middle_sq, day):
    first, last = day_edges(x, day)
    total = jnp.sum(middle + first + last, axis=0, keepdims=True)
    total_sq = jnp.sum(middle_sq + first * first + last * last, axis=0, keepdims=True)
    center = total * (1.0 / WIN)
    spread = total_sq * (1.0 / WIN) - center * center
    return center, lax.rsqrt(jnp.maximum(spread, var_floor))


def day_values(x, center, factor, day):
    row = lax.broadcasted_iota(jnp.int32, (8, x.shape[1]), 0)
    scaled = (x - center) * factor
    first = jnp.where(row >= day, scaled[:8], 0.0)
    last = jnp.where(row <= day + (WIN - 1 - (DEPTH - 8)), scaled[DEPTH - 8 :], 0.0)
    return jnp.concatenate([first, scaled[8 : DEPTH - 8], last], 0)


def halves(x):
    high = x.astype(jnp.bfloat16)
    low = (x - high.astype(jnp.float32)).astype(jnp.bfloat16)
    return high, low


def kernel(own_ref, all_ref, out_ref, high_ref, low_ref, bound_ref, lhs_ref, row_ref, sum_ref, lin_ref):
    days = out_ref.shape[0]
    mine = own_ref.shape[1]
    blocks, width = all_ref.shape[0], all_ref.shape[2]
    per_block = width // TILE
    tiles = blocks * per_block

    for at in range(0, mine, TILE):
        x = own_ref[:DEPTH, at : at + TILE].astype(jnp.float32)
        middle, middle_sq = totals(x)
        for day in range(days):
            center, inverse = day_moments(x, middle, middle_sq, day)
            w = day_values(x, center, inverse * (1.0 / (WIN * shrink_level)), day)
            row_ref[day, :, at : at + TILE] = w
            high = w.astype(jnp.bfloat16).astype(jnp.float32)
            both = jnp.concatenate([high, w - high], 0)
            for sub in range(0, TILE, 128):
                turned = both[:, sub : sub + 128].T.astype(jnp.bfloat16)
                lhs_ref[day, at + sub : at + sub + 128, :128] = turned
                lhs_ref[day, at + sub : at + sub + 128, 128:] = turned

    lin_ref[...] = jnp.zeros_like(lin_ref)

    def prepare(block, carry):
        for sub in range(per_block):
            cols = pl.ds(sub * TILE, TILE)
            dst = block * per_block + sub
            x = all_ref[block, :DEPTH, cols].astype(jnp.float32)
            signal = all_ref[block, DEPTH : DEPTH + days, cols].astype(jnp.float32)
            middle, middle_sq = totals(x)
            for day in range(days):
                s = signal[day : day + 1]
                center, inverse = day_moments(x, middle, middle_sq, day)
                v = day_values(x, center, inverse * s, day)
                lin_ref[day] += v[:, :128] + v[:, 128:]
                high, low = halves(v)
                high_ref[day, dst] = high
                low_ref[day, dst] = low
                bound_ref[day, dst] = jnp.broadcast_to(jnp.abs(s), (8, TILE))
        return carry

    lax.fori_loop(0, blocks, prepare, 0)

    def compute(*accs):
        per_unit = mine // STRIP

        def one_day(day, carry):
            def take(step):
                pair, strip = divmod(step, per_unit)
                rows = pl.ds(strip * STRIP, STRIP)
                part = None
                for unit in range(2):
                    bound = bound_ref[day, 2 * pair + unit][:1]
                    got = pltpu.matmul_pop(accs[unit * per_unit + strip])
                    kept = jnp.minimum(jnp.maximum(got, -bound), bound)
                    kept = kept[:, :128] + kept[:, 128:]
                    part = kept if part is None else part + kept
                if pair == 0:
                    sum_ref[rows, :] = part
                else:
                    sum_ref[rows, :] += part

            steps = tiles // 2 * per_unit
            for step in range(steps):
                pair, strip = divmod(step, per_unit)
                if strip == 0:
                    for unit in range(2):
                        high = high_ref[day, 2 * pair + unit]
                        low = low_ref[day, 2 * pair + unit]
                        pltpu.matmul_push_rhs(
                            jnp.concatenate([high, high, low, low], 0),
                            staging_register=pair % 2,
                            mxu_index=unit,
                        )
                lhs = lhs_ref[day, strip * STRIP : (strip + 1) * STRIP, :]
                for unit in range(2):
                    pltpu.matmul_acc_lhs(
                        accs[unit * per_unit + strip],
                        lhs,
                        load_staged_rhs=pair % 2 if strip == 0 else None,
                    )
                if step >= LAG:
                    take(step - LAG)
            for step in range(steps - LAG, steps):
                take(step)

            weight = jnp.sum(lin_ref[day], axis=1, keepdims=True)
            line = jnp.sum(row_ref[day] * weight, axis=0, keepdims=True)
            clamped = jnp.concatenate(
                [
                    jnp.sum(sum_ref[at : at + 128, :].T, axis=0, keepdims=True)
                    for at in range(0, mine, 128)
                ],
                1,
            )
            out_ref[pl.ds(day, 1), :] = (line - clamped) * shrink_level
            return carry

        lax.fori_loop(0, days, one_day, 0)

    strips = mine // STRIP
    pl.run_scoped(
        compute,
        *[pltpu.ACC(unit)((STRIP, TILE), jnp.float32) for unit in range(2) for _ in range(strips)],
    )


def filtered_rows(own, everyone, days):
    mine = own.shape[1]
    blocks, _, width = everyone.shape
    tiles = blocks * width // TILE
    vmem = pl.BlockSpec(memory_space=pltpu.VMEM)
    return pl.pallas_call(
        kernel,
        out_shape=jax.ShapeDtypeStruct((days, mine), jnp.float32),
        in_specs=[vmem, vmem],
        out_specs=vmem,
        scratch_shapes=[
            pltpu.VMEM((days, tiles, DEPTH, TILE), jnp.bfloat16),
            pltpu.VMEM((days, tiles, DEPTH, TILE), jnp.bfloat16),
            pltpu.VMEM((days, tiles, 8, TILE), jnp.float32),
            pltpu.VMEM((days, mine, TILE), jnp.bfloat16),
            pltpu.VMEM((days, DEPTH, mine), jnp.float32),
            pltpu.VMEM((mine, 128), jnp.float32),
            pltpu.VMEM((days, DEPTH, 128), jnp.float32),
        ],
        compiler_params=pltpu.CompilerParams(vmem_limit_bytes=48 << 20),
        name="filter_days",
    )(own, everyone)


def per_device(returns, signal, earlier):
    days = returns.shape[0]
    extended = history(returns, earlier)
    blank = jnp.zeros((DEPTH - extended.shape[0], extended.shape[1]), extended.dtype)
    own = jnp.concatenate([extended, blank, signal], 0)
    copies = jnp.broadcast_to(own, (lax.axis_size("asset"), *own.shape))
    everyone = lax.all_to_all(copies, "asset", split_axis=0, concat_axis=0, tiled=True)
    return filtered_rows(own, everyone, days)


def solution(mesh):
    in_specs = (P("tm", "asset"), P("tm", "asset"), P(None, "asset"))
    out_specs = P("tm", "asset")
    return jax.shard_map(
        per_device, mesh=mesh, in_specs=in_specs, out_specs=out_specs, check_vma=False
    )
```

time: 165 us -> 87.3 us (0.53)
  matrix products: 80.2 us -> 0 us
  Pallas kernels: 0 us -> 23.1 us
  blocking collectives: 0 us -> 17.5 us
  waiting for transfers between devices: 46.4 us -> 33.6 us
  loops' own time: 11.4 us -> 0 us
  local copies, waits for them, and re-layouts: 6.41 us -> 0.94 us
  starting transfers between devices: 12.9 us -> 7.67 us
  other arithmetic: 6.28 us -> 3.76 us
    dot_general x4 -> x0, matrix products: 80.2 us -> none  [one_day(): return jnp.dot(shrunk, day_signal, preferred_element_type=jnp.float32)]
    pallas_call x0 -> x1, Pallas kernels: none -> 23.1 us  [filtered_rows(): pl.pallas_call(kernel, out_shape=jax.ShapeDtypeStruct((days, mine), jnp.f...]
    all_to_all x0 -> x1, blocking collectives: none -> 17.5 us  [per_device(): lax.all_to_all(copies, 'asset', split_axis=0, concat_axis=0, tiled=True)]
    all_to_all x1 -> x0, waiting for transfers between devices: 12.3 us -> none  [copy_for_each(): return lax.all_to_all(copies, axis, split_axis=0, concat_axis=0, tiled=True)]
    another operation x1 -> x0, loops' own time: 11.4 us -> none  [contribution(): return lax.map(one_day, jnp.arange(signal_cols.shape[0], dtype=jnp.int32))]
    all_to_all x1 -> x0, starting transfers between devices: 5.26 us -> none  [copy_for_each(): return lax.all_to_all(copies, axis, split_axis=0, concat_axis=0, tiled=True)]
    reduce_sum x8 -> x0, other arithmetic: 2.47 us -> none  [moments(): center = jnp.mean(values, axis=0)]
    dynamic_slice x4 -> x0, local copies, waits for them, and re-layouts: 2.32 us -> none  [contribution(): return lax.map(one_day, jnp.arange(signal_cols.shape[0], dtype=jnp.int32))]
  transfers between devices with their start and end apart: 5 -> 4, of which waited for: 5 -> 4; matrix products, arithmetic and copies ran while one was open for 0% -> 0% of each run, Pallas kernels for 0% -> 0%
where the time goes in v1:
time: 87.3 us; the launch traced here: 86.7 us
  waiting for transfers between devices  33.6 us (38%)
  Pallas kernels  23.1 us (26%)
  blocking collectives  17.5 us (20%)
  starting transfers between devices  7.67 us (9%)
  other arithmetic  3.76 us (4%)
  local copies, waits for them, and re-layouts  0.94 us (1%)
    ppermute x4, waiting for transfers between devices, passed_along(): return lax.ppermute(value, axis, pairs)  33.6 us
    pallas_call x1, Pallas kernels, filtered_rows(): pl.pallas_call(kernel, out_shape=jax.ShapeDtypeStruct((days, mine), jnp.f...  23.1 us
    all_to_all x1, blocking collectives, per_device(): lax.all_to_all(copies, 'asset', split_axis=0, concat_axis=0, tiled=True)  17.5 us
    ppermute x4, starting transfers between devices, passed_along(): return lax.ppermute(value, axis, pairs)  7.67 us
    concatenate x3, other arithmetic, history(): stacked = jnp.concatenate([moved, stacked], 0)  2.13 us
  transfers between devices with their start and end apart: 4, of which 4 were waited for; matrix products, arithmetic and copies ran while one was open for 0% of the time, Pallas kernels for 0%

profile of v1, /device:TPU:16, one launch (start us, length us, event | category | flops | bytes accessed | tf_op | source)
XLA Modules:
  0.0 86.7 jit_solution(7590209815431062788)
XLA Ops:
  0.0 1.9 %collective-permute-start = (bf16[4,1024]{1,0:T(4,128)(2,1)}, bf16[4,1024]{1,0:T(4,128)(2,1)S(1)}, u32[]{:S(2)}, u32[]{:S(2)}) collective-permute-start(bf16[4,1024]{1,0:T(4,128)(2,1)} %param.3), channel_id=1, source_target_pairs={{0,8},{8,16},{16,24},{24,32},{32,40},{40,48},{48,56},{56,64},{64,7... | collective-permute-start | bytes 24584 | tf_op jit(solution)/shard_map/ppermute | solution.py:22
  1.9 6.9 %collective-permute-done = bf16[4,1024]{1,0:T(4,128)(2,1)S(1)} collective-permute-done((bf16[4,1024]{1,0:T(4,128)(2,1)}, bf16[4,1024]{1,0:T(4,128)(2,1)S(1)}, u32[]{:S(2)}, u32[]{:S(2)}) %collective-permute-start) | collective-permute-done | bytes 8224 | tf_op jit(solution)/shard_map/ppermute | solution.py:22
  8.8 0.7 pad_maximum_fusion.3
  9.5 1.9 %collective-permute-start.1 = (bf16[8,1024]{1,0:T(8,128)(2,1)S(1)}, bf16[8,1024]{1,0:T(8,128)(2,1)S(1)}, u32[]{:S(2)}, u32[]{:S(2)}) collective-permute-start(bf16[8,1024]{1,0:T(8,128)(2,1)S(1)} %pad_maximum_fusion.3), channel_id=1, source_target_pairs={{0,16},{8,24},{16,32},{24,40},{32,48},{40,56},{48,64},{56,72},{64,... | collective-permute-start | bytes 49160 | tf_op jit(solution)/shard_map/ppermute | solution.py:22
  11.4 7.3 %collective-permute-done.1 = bf16[8,1024]{1,0:T(8,128)(2,1)S(1)} collective-permute-done((bf16[8,1024]{1,0:T(8,128)(2,1)S(1)}, bf16[8,1024]{1,0:T(8,128)(2,1)S(1)}, u32[]{:S(2)}, u32[]{:S(2)}) %collective-permute-start.1) | collective-permute-done | bytes 16416 | tf_op jit(solution)/shard_map/ppermute | solution.py:22
  18.7 0.7 pad_maximum_fusion.2
  19.5 1.9 %collective-permute-start.2 = (bf16[16,1024]{1,0:T(8,128)(2,1)S(1)}, bf16[16,1024]{1,0:T(8,128)(2,1)S(1)}, u32[]{:S(2)}, u32[]{:S(2)}) collective-permute-start(bf16[16,1024]{1,0:T(8,128)(2,1)S(1)} %pad_maximum_fusion.2), channel_id=1, source_target_pairs={{0,32},{8,40},{16,48},{24,56},{32,64},{40,72},{48,80},{56,88},{64,... | collective-permute-start | bytes 98312 | tf_op jit(solution)/shard_map/ppermute | solution.py:22
  21.4 0.1 pad.2.clone
  21.5 8.3 %collective-permute-done.2 = bf16[16,1024]{1,0:T(8,128)(2,1)S(1)} collective-permute-done((bf16[16,1024]{1,0:T(8,128)(2,1)S(1)}, bf16[16,1024]{1,0:T(8,128)(2,1)S(1)}, u32[]{:S(2)}, u32[]{:S(2)}) %collective-permute-start.2) | collective-permute-done | bytes 32800 | tf_op jit(solution)/shard_map/ppermute | solution.py:22
  29.8 0.7 pad_maximum_fusion.1
  30.5 1.9 %collective-permute-start.3 = (bf16[32,1024]{1,0:T(8,128)(2,1)S(1)}, bf16[32,1024]{1,0:T(8,128)(2,1)S(1)}, u32[]{:S(2)}, u32[]{:S(2)}) collective-permute-start(bf16[32,1024]{1,0:T(8,128)(2,1)S(1)} %pad_maximum_fusion.1), channel_id=1, source_target_pairs={{0,64},{8,72},{16,80},{24,88},{32,96},{40,104},{48,112},{56,120},{... | collective-permute-start | bytes 196616 | tf_op jit(solution)/shard_map/ppermute | solution.py:22
  32.4 11.1 %collective-permute-done.3 = bf16[32,1024]{1,0:T(8,128)(2,1)S(1)} collective-permute-done((bf16[32,1024]{1,0:T(8,128)(2,1)S(1)}, bf16[32,1024]{1,0:T(8,128)(2,1)S(1)}, u32[]{:S(2)}, u32[]{:S(2)}) %collective-permute-start.3) | collective-permute-done | bytes 65568 | tf_op jit(solution)/shard_map/ppermute | solution.py:22
  43.6 0.7 concatenate.25
  44.3 0.8 fusion
  45.1 0.8 pad_maximum_fusion.own_ref
  45.9 0.1 broadcast_in_dim.18
  46.1 17.5 %all_to_all.5.all_ref = bf16[8,68,1024]{2,1,0:T(8,128)(2,1)S(1)} all-to-all(bf16[8,68,1024]{2,1,0:T(8,128)(2,1)S(1)} %broadcast_in_dim.18), channel_id=1, replica_groups=mesh['tm'=32,'asset'=8] {'asset'}, dimensions={0} | all-to-all | bytes 2228224 | tf_op jit(solution)/shard_map/all_to_all | solution.py:220
  63.6 23.1 %filter_days.1 = f32[4,1024]{1,0:T(4,128)} custom-call(bf16[68,1024]{1,0:T(8,128)(2,1)S(1)} %pad_maximum_fusion.own_ref, bf16[8,68,1024]{2,1,0:T(8,128)(2,1)S(1)} %all_to_all.5.all_ref), custom_call_target="tpu_custom_call" | custom-call | tf_op jit(solution)/shard_map/filter_days/pallas_call | solution.py:195
  (1 shorter events, 0.0 us)
Async XLA Ops:
  0.0 8.8 %collective-permute-start = (bf16[4,1024]{1,0:T(4,128)(2,1)}, bf16[4,1024]{1,0:T(4,128)(2,1)S(1)}, u32[]{:S(2)}, u32[]{:S(2)}) collective-permute-start(bf16[4,1024]{1,0:T(4,128)(2,1)} %param.3), channel_id=1, source_target_pairs={{0,8},{8,16},{16,24},{24,32},{32,40},{40,48},{48,56},{56,64},{64,7... | collective-permute-start | bytes 24584 | tf_op jit(solution)/shard_map/ppermute | solution.py:22
  9.5 9.2 %collective-permute-start.1 = (bf16[8,1024]{1,0:T(8,128)(2,1)S(1)}, bf16[8,1024]{1,0:T(8,128)(2,1)S(1)}, u32[]{:S(2)}, u32[]{:S(2)}) collective-permute-start(bf16[8,1024]{1,0:T(8,128)(2,1)S(1)} %pad_maximum_fusion.3), channel_id=1, source_target_pairs={{0,16},{8,24},{16,32},{24,40},{32,48},{40,56},{48,64},{56,72},{64,... | collective-permute-start | bytes 49160 | tf_op jit(solution)/shard_map/ppermute | solution.py:22
  19.5 10.3 %collective-permute-start.2 = (bf16[16,1024]{1,0:T(8,128)(2,1)S(1)}, bf16[16,1024]{1,0:T(8,128)(2,1)S(1)}, u32[]{:S(2)}, u32[]{:S(2)}) collective-permute-start(bf16[16,1024]{1,0:T(8,128)(2,1)S(1)} %pad_maximum_fusion.2), channel_id=1, source_target_pairs={{0,32},{8,40},{16,48},{24,56},{32,64},{40,72},{48,80},{56,88},{64,... | collective-permute-start | bytes 98312 | tf_op jit(solution)/shard_map/ppermute | solution.py:22
  30.5 13.1 %collective-permute-start.3 = (bf16[32,1024]{1,0:T(8,128)(2,1)S(1)}, bf16[32,1024]{1,0:T(8,128)(2,1)S(1)}, u32[]{:S(2)}, u32[]{:S(2)}) collective-permute-start(bf16[32,1024]{1,0:T(8,128)(2,1)S(1)} %pad_maximum_fusion.1), channel_id=1, source_target_pairs={{0,64},{8,72},{16,80},{24,88},{32,96},{40,104},{48,112},{56,120},{... | collective-permute-start | bytes 196616 | tf_op jit(solution)/shard_map/ppermute | solution.py:22

commit v2 on v1

--- a/solution.py
+++ b/solution.py
@@ -11,67 +11,241 @@
 TILE = 256
 STRIP = 128
 LAG = 4
+BLOCKS = 16
 
 var_floor = 0.05
 shrink_level = 0.1
 
 
-def passed_along(value, axis, by):
-    peers = lax.axis_size(axis)
-    pairs = [(i, i + by) for i in range(peers) if 0 <= i + by < peers]
-    return lax.ppermute(value, axis, pairs)
-
-
-def history(block_rows, earlier_rows):
-    day_dev = block_rows.shape[0]
-    position = lax.axis_index("tm")
-    span = HIST + day_dev
-    blocks_needed = -(-HIST // day_dev)
-    stacked = block_rows
-    for level in range(blocks_needed.bit_length()):
-        moved = passed_along(stacked, "tm", 1 << level)
-        stacked = jnp.concatenate([moved, stacked], 0)
-    tail_rows = stacked[stacked.shape[0] - span :]
-    padded = jnp.concatenate(
-        [earlier_rows, jnp.zeros((span, earlier_rows.shape[1]), earlier_rows.dtype)], 0
-    )
-    filler = lax.dynamic_slice_in_dim(padded, position * day_dev, span, 0)
-    offsets = position * day_dev - HIST + jnp.arange(span, dtype=jnp.int32)
-    return jnp.where((offsets < 0)[:, None], filler, tail_rows)
+def odd_place(slot):
+    return 1 + slot // 2
+
+
+def even_place(slot):
+    return 9 + slot // 2
+
+
+def gather_kernel(returns_ref, signal_ref, old_ref, out_ref, send_far, got_far, send_peer, got_peer, send_edge, got_edge, send_twin, got_twin):
+    time, own = lax.axis_index("tm"), lax.axis_index("asset")
+    times, peers = lax.axis_size("tm"), lax.axis_size("asset")
+    core = lax.rem(time, 2)
+    twin = time + 1 - 2 * core
+    even, odd = core == 0, core == 1
+    reach = BLOCKS - 1
+
+    def peer(step):
+        return lax.rem(own + step, peers)
+
+    def at(t, a):
+        return dict(device_id=(t, a), device_id_type=pl.DeviceIdType.MESH)
+
+    barrier = pltpu.get_barrier_semaphore()
+
+    def greet(valid, t, a):
+        @pl.when(valid)
+        def _():
+            pl.semaphore_signal(barrier, inc=1, **at(t, a))
+
+    count = peers
+    for back in range(2, reach, 2):
+        greet(time + back < times, time + back, own)
+        greet(time - back >= 0, time - back, own)
+        count += (time + back < times).astype(jnp.int32) + (time - back >= 0).astype(jnp.int32)
+    forward = jnp.logical_and(odd, time + reach < times)
+    backward = jnp.logical_and(even, time - reach >= 0)
+    greet(forward, time + reach, own)
+    greet(backward, time - reach, own)
+    count += forward.astype(jnp.int32) + backward.astype(jnp.int32)
+    for step in range(1, peers):
+        pl.semaphore_signal(barrier, inc=1, **at(time, peer(step)))
+    pl.semaphore_signal(barrier, inc=1, **at(twin, own))
+    pl.semaphore_wait(barrier, count)
+
+    def far(back, place, to):
+        return pltpu.make_async_remote_copy(
+            src_ref=returns_ref,
+            dst_ref=out_ref.at[own, place],
+            send_sem=send_far.at[back // 2],
+            recv_sem=got_far.at[back // 2],
+            **at(to, own),
+        )
+
+    for back in range(2, reach, 2):
+        @pl.when(time + back < times)
+        def _(back=back):
+            far(back, odd_place(reach - back), time + back).start()
+
+    @pl.when(forward)
+    def _():
+        pltpu.make_async_remote_copy(
+            src_ref=returns_ref,
+            dst_ref=out_ref.at[own, even_place(0)],
+            send_sem=send_far.at[0],
+            recv_sem=got_far.at[0],
+            **at(time + reach, own),
+        ).start()
+
+    out_ref[own, 0] = signal_ref[...]
+    out_ref[own, odd_place(reach)] = returns_ref[...]
+    for slot in range(1, reach, 2):
+        @pl.when(time + slot < reach)
+        def _(slot=slot):
+            out_ref[own, odd_place(slot)] = old_ref[time + slot]
+
+    @pl.when(jnp.logical_and(even, time < reach))
+    def _():
+        out_ref[own, even_place(0)] = old_ref[time]
+
+    for back in range(2, reach, 2):
+        @pl.when(time - back >= 0)
+        def _(back=back):
+            far(back, odd_place(reach - back), time).wait_recv()
+
+        @pl.when(time + back < times)
+        def _(back=back):
+            far(back, odd_place(reach - back), time).wait_send()
+
+    def edge_far():
+        return pltpu.make_async_remote_copy(
+            src_ref=returns_ref,
+            dst_ref=out_ref.at[own, even_place(0)],
+            send_sem=send_far.at[0],
+            recv_sem=got_far.at[0],
+            **at(time, own),
+        )
+
+    @pl.when(backward)
+    def _():
+        edge_far().wait_recv()
+
+    @pl.when(forward)
+    def _():
+        edge_far().wait_send()
+
+    half = pl.ds(0, 9)
+
+    def across(step, a):
+        return pltpu.make_async_remote_copy(
+            src_ref=out_ref.at[a, half],
+            dst_ref=out_ref.at[a, half],
+            send_sem=send_peer.at[step],
+            recv_sem=got_peer.at[step],
+            **at(time, peer(step)),
+        )
+
+    def across_edge(step, a):
+        return pltpu.make_async_remote_copy(
+            src_ref=out_ref.at[a, even_place(0)],
+            dst_ref=out_ref.at[a, even_place(0)],
+            send_sem=send_edge.at[step],
+            recv_sem=got_edge.at[step],
+            **at(time, peer(step)),
+        )
+
+    def over(step, a, low):
+        size = 7 + low
+        return pltpu.make_async_remote_copy(
+            src_ref=out_ref.at[a, pl.ds(1, size)],
+            dst_ref=out_ref.at[a, pl.ds(10 - low, size)],
+            send_sem=send_twin.at[step],
+            recv_sem=got_twin.at[step],
+            **at(twin, own),
+        )
+
+    for step in range(1, peers):
+        across(step, own).start()
+
+        @pl.when(even)
+        def _(step=step):
+            across_edge(step, own).start()
+
+    def hand_over(step, a):
+        @pl.when(even)
+        def _():
+            over(step, a, 1).start()
+
+        @pl.when(odd)
+        def _():
+            over(step, a, 0).start()
+
+    hand_over(0, own)
+    for step in range(1, peers):
+        source = peer(peers - step)
+        across(step, source).wait_recv()
+        hand_over(step, source)
+
+    for step in range(peers):
+        source = peer(peers - step)
+
+        @pl.when(even)
+        def _(step=step, source=source):
+            over(step, source, 0).wait_recv()
+            over(step, source, 1).wait_send()
+
+        @pl.when(odd)
+        def _(step=step, source=source):
+            over(step, source, 1).wait_recv()
+            over(step, source, 0).wait_send()
+
+        if step:
+            across(step, own).wait_send()
+
+            @pl.when(even)
+            def _(step=step, source=source):
+                across_edge(step, source).wait_recv()
+                across_edge(step, own).wait_send()
+
+
+def gathered(returns, signal, earlier):
+    days, mine = returns.shape
+    peers = lax.axis_size("asset")
+    old = jnp.pad(earlier, ((1, 0), (0, 0))).reshape(BLOCKS - 1, days, mine)
+    vmem = pl.BlockSpec(memory_space=pltpu.VMEM)
+    dma = pltpu.SemaphoreType.DMA
+    return pl.pallas_call(
+        gather_kernel,
+        out_shape=jax.ShapeDtypeStruct((peers, BLOCKS + 1, days, mine), returns.dtype),
+        in_specs=[vmem] * 3,
+        out_specs=vmem,
+        scratch_shapes=[dma((BLOCKS // 2,))] * 2 + [dma((peers,))] * 6,
+        compiler_params=pltpu.CompilerParams(
+            collective_id=0, has_side_effects=True, vmem_limit_bytes=8 << 20
+        ),
+        name="gather_windows",
+    )(returns, signal, old)
 
 
 def totals(x):
-    middle = x[8:16]
-    middle_sq = middle * middle
-    for at in range(16, DEPTH - 8, 8):
+    middle = middle_sq = None
+    for at in range(0, DEPTH, 8):
+        if at in (24, 32):
+            continue
         part = x[at : at + 8]
-        middle = middle + part
-        middle_sq = middle_sq + part * part
+        middle = part if middle is None else middle + part
+        middle_sq = part * part if middle_sq is None else middle_sq + part * part
     return middle, middle_sq
 
 
 def day_edges(x, day):
     row = lax.broadcasted_iota(jnp.int32, (8, x.shape[1]), 0)
-    first = jnp.where(row >= day, x[:8], 0.0)
-    last = jnp.where(row <= day + (WIN - 1 - (DEPTH - 8)), x[DEPTH - 8 :], 0.0)
-    return first, last
+    newest = jnp.where(row <= day + 4, x[24:32], 0.0)
+    oldest = jnp.where(row >= day + 1, x[32:40], 0.0)
+    return newest, oldest
 
 
 def day_moments(x, middle, middle_sq, day):
-    first, last = day_edges(x, day)
-    total = jnp.sum(middle + first + last, axis=0, keepdims=True)
-    total_sq = jnp.sum(middle_sq + first * first + last * last, axis=0, keepdims=True)
+    newest, oldest = day_edges(x, day)
+    total = jnp.sum(middle + newest + oldest, axis=0, keepdims=True)
+    total_sq = jnp.sum(middle_sq + newest * newest + oldest * oldest, axis=0, keepdims=True)
     center = total * (1.0 / WIN)
     spread = total_sq * (1.0 / WIN) - center * center
     return center, lax.rsqrt(jnp.maximum(spread, var_floor))
 
 
 def day_values(x, center, factor, day):
-    row = lax.broadcasted_iota(jnp.int32, (8, x.shape[1]), 0)
     scaled = (x - center) * factor
-    first = jnp.where(row >= day, scaled[:8], 0.0)
-    last = jnp.where(row <= day + (WIN - 1 - (DEPTH - 8)), scaled[DEPTH - 8 :], 0.0)
-    return jnp.concatenate([first, scaled[8 : DEPTH - 8], last], 0)
+    newest, oldest = day_edges(scaled, day)
+    return jnp.concatenate([scaled[:24], newest, oldest, scaled[40:]], 0)
 
 
 def halves(x):
@@ -80,15 +254,21 @@
     return high, low
 
 
-def kernel(own_ref, all_ref, out_ref, high_ref, low_ref, bound_ref, lhs_ref, row_ref, sum_ref, lin_ref):
+def window(all_ref, block, cols):
+    x = all_ref[block, 1:, :, cols].astype(jnp.float32)
+    return x.reshape(DEPTH, TILE)
+
+
+def kernel(all_ref, out_ref, high_ref, low_ref, bound_ref, lhs_ref, row_ref, sum_ref, lin_ref):
     days = out_ref.shape[0]
-    mine = own_ref.shape[1]
-    blocks, width = all_ref.shape[0], all_ref.shape[2]
+    blocks, width = all_ref.shape[0], all_ref.shape[3]
+    mine = width
+    own = lax.axis_index("asset")
     per_block = width // TILE
     tiles = blocks * per_block
 
     for at in range(0, mine, TILE):
-        x = own_ref[:DEPTH, at : at + TILE].astype(jnp.float32)
+        x = window(all_ref, own, pl.ds(at, TILE))
         middle, middle_sq = totals(x)
         for day in range(days):
             center, inverse = day_moments(x, middle, middle_sq, day)
@@ -107,8 +287,8 @@
         for sub in range(per_block):
             cols = pl.ds(sub * TILE, TILE)
             dst = block * per_block + sub
-            x = all_ref[block, :DEPTH, cols].astype(jnp.float32)
-            signal = all_ref[block, DEPTH : DEPTH + days, cols].astype(jnp.float32)
+            x = window(all_ref, block, cols)
+            signal = all_ref[block, 0, :, cols].astype(jnp.float32)
             middle, middle_sq = totals(x)
             for day in range(days):
                 s = signal[day : day + 1]
@@ -187,15 +367,15 @@
     )
 
 
-def filtered_rows(own, everyone, days):
-    mine = own.shape[1]
-    blocks, _, width = everyone.shape
+def filtered_rows(everyone):
+    blocks, _, days, width = everyone.shape
+    mine = width
     tiles = blocks * width // TILE
     vmem = pl.BlockSpec(memory_space=pltpu.VMEM)
     return pl.pallas_call(
         kernel,
         out_shape=jax.ShapeDtypeStruct((days, mine), jnp.float32),
-        in_specs=[vmem, vmem],
+        in_specs=[vmem],
         out_specs=vmem,
         scratch_shapes=[
             pltpu.VMEM((days, tiles, DEPTH, TILE), jnp.bfloat16),
@@ -208,17 +388,11 @@
         ],
         compiler_params=pltpu.CompilerParams(vmem_limit_bytes=48 << 20),
         name="filter_days",
-    )(own, everyone)
+    )(everyone)
 
 
 def per_device(returns, signal, earlier):
-    days = returns.shape[0]
-    extended = history(returns, earlier)
-    blank = jnp.zeros((DEPTH - extended.shape[0], extended.shape[1]), extended.dtype)
-    own = jnp.concatenate([extended, blank, signal], 0)
-    copies = jnp.broadcast_to(own, (lax.axis_size("asset"), *own.shape))
-    everyone = lax.all_to_all(copies, "asset", split_axis=0, concat_axis=0, tiled=True)
-    return filtered_rows(own, everyone, days)
+    return filtered_rows(gathered(returns, signal, earlier))
 
 
 def solution(mesh):

time: 87.3 us -> 51.9 us (0.59)
  waiting for transfers between devices: 33.6 us -> 0 us
  Pallas kernels: 23.1 us -> 48.7 us
  blocking collectives: 17.5 us -> 0 us
  starting transfers between devices: 7.67 us -> 0 us
  other arithmetic: 3.76 us -> 0 us
  local copies, waits for them, and re-layouts: 0.94 us -> 2.39 us
    ppermute x4 -> x0, waiting for transfers between devices: 33.6 us -> none  [passed_along(): return lax.ppermute(value, axis, pairs)]
    pallas_call x0 -> x1, Pallas kernels: none -> 24.9 us  [gathered(): pl.pallas_call(gather_kernel, out_shape=jax.ShapeDtypeStruct((peers, BLOC...]
    all_to_all x1 -> x0, blocking collectives: 17.5 us -> none  [per_device(): lax.all_to_all(copies, 'asset', split_axis=0, concat_axis=0, tiled=True)]
    ppermute x4 -> x0, starting transfers between devices: 7.67 us -> none  [passed_along(): return lax.ppermute(value, axis, pairs)]
    concatenate x4 -> x0, other arithmetic: 2.92 us -> none  [the longest x3 2.13 us: history(): stacked = jnp.concatenate([moved, stacked], 0)]
    unnamed x0 -> x4, local copies, waits for them, and re-layouts: none -> 1.39 us
    pad x0 -> x1, local copies, waits for them, and re-layouts: none -> 0.94 us  [gathered(): old = jnp.pad(earlier, ((1, 0), (0, 0))).reshape(BLOCKS - 1, days, mine)]
  transfers between devices with their start and end apart: 4 -> 0, of which waited for: 4 -> 0; matrix products, arithmetic and copies ran while one was open for 0% -> 0% of each run, Pallas kernels for 0% -> 0%
where the time goes in v2:
time: 51.9 us; the launch traced here: 51.1 us
  Pallas kernels  48.7 us (94%)
  local copies, waits for them, and re-layouts  2.39 us (5%)
    pallas_call x1, Pallas kernels, gathered(): pl.pallas_call(gather_kernel, out_shape=jax.ShapeDtypeStruct((peers, BLOC...  24.9 us
    pallas_call x1, Pallas kernels, filtered_rows(): pl.pallas_call(kernel, out_shape=jax.ShapeDtypeStruct((days, mine), jnp.f...  23.8 us
    unnamed x4, local copies, waits for them, and re-layouts  1.39 us

profile of v2, /device:TPU:16, one launch (start us, length us, event | category | flops | bytes accessed | tf_op | source)
XLA Modules:
  0.0 51.1 jit_solution(14616548944823760839)
XLA Ops:
  0.0 0.9 %pad.4 = bf16[60,1024]{1,0:T(8,128)(2,1)S(1)} pad(bf16[59,1024]{1,0:T(8,128)(2,1)} %param.5, bf16[]{:T(256)} %constant.2.clone.1), padding=1_0x0_0 | pad | bytes 243714 | tf_op jit(solution)/shard_map/jit(_pad)/pad | solution.py:202
  0.9 0.1 reshape.3.old_ref
  1.0 0.0 copy-start
  1.0 0.7 %copy-done = bf16[4,1024]{1,0:T(4,128)(2,1)S(1)} copy-done((bf16[4,1024]{1,0:T(4,128)(2,1)S(1)}, bf16[4,1024]{1,0:T(4,128)(2,1)}, u32[]{:S(2)}) %copy-start) | copy-done | bytes 8216
  1.7 0.0 copy-start.1
  1.7 0.7 %copy-done.1 = bf16[4,1024]{1,0:T(4,128)(2,1)S(1)} copy-done((bf16[4,1024]{1,0:T(4,128)(2,1)S(1)}, bf16[4,1024]{1,0:T(4,128)(2,1)}, u32[]{:S(2)}) %copy-start.1) | copy-done | bytes 8216
  2.4 24.9 %gather_windows.1.all_ref = bf16[8,17,4,1024]{3,2,1,0:T(4,128)(2,1)S(1)} custom-call(bf16[4,1024]{1,0:T(4,128)(2,1)S(1)} %copy-done, bf16[4,1024]{1,0:T(4,128)(2,1)S(1)} %copy-done.1, bf16[15,4,1024]{2,1,0:T(4,128)(2,1)S(1)} %reshape.3.old_ref), custom_call_target="tpu_custom_call" | custom-call | tf_op jit(solution)/shard_map/gather_windows/pallas_call | solution.py:205
  27.3 23.8 %filter_days.1 = f32[4,1024]{1,0:T(4,128)} custom-call(bf16[8,17,4,1024]{3,2,1,0:T(4,128)(2,1)S(1)} %gather_windows.1.all_ref), custom_call_target="tpu_custom_call" | custom-call | tf_op jit(solution)/shard_map/filter_days/pallas_call | solution.py:375
Async XLA Ops:
  1.0 0.7 %copy-start = (bf16[4,1024]{1,0:T(4,128)(2,1)S(1)}, bf16[4,1024]{1,0:T(4,128)(2,1)}, u32[]{:S(2)}) copy-start(bf16[4,1024]{1,0:T(4,128)(2,1)} %returns_ref.1) | copy-start | bytes 24580
  1.7 0.7 %copy-start.1 = (bf16[4,1024]{1,0:T(4,128)(2,1)S(1)}, bf16[4,1024]{1,0:T(4,128)(2,1)}, u32[]{:S(2)}) copy-start(bf16[4,1024]{1,0:T(4,128)(2,1)} %signal_ref.1) | copy-start | bytes 24580

commit v3 on v0

v3 whole, which is shorter than its diff:
```python
import jax
import jax.numpy as jnp
from jax import lax
from jax.experimental import pallas as pl
from jax.experimental.pallas import tpu as pltpu
from jax.sharding import PartitionSpec as P

WIN = 60
HIST = 59
DEPTH = 64
TILE = 256
STRIP = 128
LAG = 4
BLOCKS = 16

var_floor = 0.05
shrink_level = 0.1


def totals(x):
    middle = middle_sq = None
    for at in range(0, DEPTH, 8):
        if at in (24, 32):
            continue
        part = x[at : at + 8]
        middle = part if middle is None else middle + part
        middle_sq = part * part if middle_sq is None else middle_sq + part * part
    return middle, middle_sq


def day_edges(x, day):
    row = lax.broadcasted_iota(jnp.int32, (8, x.shape[1]), 0)
    newest = jnp.where(row <= day + 4, x[24:32], 0.0)
    oldest = jnp.where(row >= day + 1, x[32:40], 0.0)
    return newest, oldest


def day_moments(x, middle, middle_sq, day):
    newest, oldest = day_edges(x, day)
    total = jnp.sum(middle + newest + oldest, axis=0, keepdims=True)
    total_sq = jnp.sum(middle_sq + newest * newest + oldest * oldest, axis=0, keepdims=True)
    center = total * (1.0 / WIN)
    spread = total_sq * (1.0 / WIN) - center * center
    return center, lax.rsqrt(jnp.maximum(spread, var_floor))


def day_values(x, center, factor, day):
    scaled = (x - center) * factor
    newest, oldest = day_edges(scaled, day)
    return jnp.concatenate([scaled[:24], newest, oldest, scaled[40:]], 0)


def halves(x):
    high = x.astype(jnp.bfloat16)
    low = (x - high.astype(jnp.float32)).astype(jnp.bfloat16)
    return high, low


def odd_place(slot):
    return 1 + slot // 2


def even_place(slot):
    return 9 + slot // 2


def window(store_ref, block, cols):
    x = store_ref[block, 1:, :, cols].astype(jnp.float32)
    return x.reshape(DEPTH, TILE)


def kernel(
    returns_ref, signal_ref, earlier_ref, out_ref,
    store_ref, old_ref, before_ref, high_ref, low_ref, bound_ref, lhs_ref, row_ref, sum_ref, lin_ref, x_ref, tot_ref,
    fill_sem, send_far, got_far, send_peer, got_peer, send_edge, got_edge, send_twin, got_twin,
):
    days, mine = out_ref.shape
    time, own = lax.axis_index("tm"), lax.axis_index("asset")
    times, peers = lax.axis_size("tm"), lax.axis_size("asset")
    core = lax.rem(time, 2)
    twin = time + 1 - 2 * core
    even, odd = core == 0, core == 1
    reach = BLOCKS - 1
    column, side = own // 2, lax.rem(own, 2)

    def at(t, a):
        return dict(device_id=(t, a), device_id_type=pl.DeviceIdType.MESH)

    def peer(step, sign):
        along = (0, 0, 1, 3, 2, 1, 3, 2)[step]
        other = (0, 1, 0, 0, 0, 1, 1, 1)[step]
        flipped = 1 - side if other else side
        return 2 * lax.rem(column + (along if sign > 0 else peers // 2 - along), peers // 2) + flipped

    fills = [
        pltpu.make_async_copy(returns_ref, store_ref.at[0, odd_place(reach)], fill_sem.at[0]),
        pltpu.make_async_copy(signal_ref, store_ref.at[0, 0], fill_sem.at[1]),
        pltpu.make_async_copy(earlier_ref, before_ref, fill_sem.at[2]),
    ]
    for fill in fills:
        fill.start()

    barrier = pltpu.get_barrier_semaphore()

    def greet(valid, t, a):
        @pl.when(valid)
        def _():
            pl.semaphore_signal(barrier, inc=1, **at(t, a))

    count = peers
    forward = jnp.logical_and(odd, time + reach < times)
    backward = jnp.logical_and(even, time - reach >= 0)
    greet(forward, time + reach, own)
    greet(backward, time - reach, own)
    count += forward.astype(jnp.int32) + backward.astype(jnp.int32)
    for back in range(reach - 1, 0, -2):
        greet(time + back < times, time + back, own)
        greet(time - back >= 0, time - back, own)
        count += (time + back < times).astype(jnp.int32) + (time - back >= 0).astype(jnp.int32)
    for step in range(1, peers):
        pl.semaphore_signal(barrier, inc=1, **at(time, peer(step, 1)))
    pl.semaphore_signal(barrier, inc=1, **at(twin, own))

    for fill in fills:
        fill.wait()
    shifted = jnp.concatenate(
        [jnp.zeros((1, mine), jnp.float32), before_ref[...].astype(jnp.float32)], 0
    )
    old_ref[...] = shifted.reshape(reach, days, mine).astype(jnp.bfloat16)
    for slot in range(1, reach, 2):
        @pl.when(time + slot < reach)
        def _(slot=slot):
            store_ref[0, odd_place(slot)] = old_ref[time + slot]

    @pl.when(jnp.logical_and(even, time < reach))
    def _():
        store_ref[0, even_place(0)] = old_ref[time]

    sum_ref[...] = jnp.zeros_like(sum_ref)
    lin_ref[...] = jnp.zeros_like(lin_ref)

    pl.semaphore_wait(barrier, count)

    def far(back, place, to):
        return pltpu.make_async_remote_copy(
            src_ref=store_ref.at[0, odd_place(reach)],
            dst_ref=store_ref.at[0, place],
            send_sem=send_far.at[back % reach // 2],
            recv_sem=got_far.at[back % reach // 2],
            **at(to, own),
        )

    @pl.when(forward)
    def _():
        far(reach, even_place(0), time + reach).start()

    for back in range(reach - 1, 0, -2):
        @pl.when(time + back < times)
        def _(back=back):
            far(back, odd_place(reach - back), time + back).start()

    for back in range(2, reach, 2):
        @pl.when(time - back >= 0)
        def _(back=back):
            far(back, odd_place(reach - back), time).wait_recv()

    def across(step, to):
        half = pl.ds(0, 9)
        return pltpu.make_async_remote_copy(
            src_ref=store_ref.at[0, half],
            dst_ref=store_ref.at[step, half],
            send_sem=send_peer.at[step],
            recv_sem=got_peer.at[step],
            **at(time, to),
        )

    def across_edge(step, to):
        return pltpu.make_async_remote_copy(
            src_ref=store_ref.at[0, even_place(0)],
            dst_ref=store_ref.at[step, even_place(0)],
            send_sem=send_edge.at[step],
            recv_sem=got_edge.at[step],
            **at(time, to),
        )

    def over(step, low):
        size = 7 + low
        return pltpu.make_async_remote_copy(
            src_ref=store_ref.at[step, pl.ds(1, size)],
            dst_ref=store_ref.at[step, pl.ds(10 - low, size)],
            send_sem=send_twin.at[step],
            recv_sem=got_twin.at[step],
            **at(twin, own),
        )

    def hand_over(step):
        @pl.when(even)
        def _():
            over(step, 1).start()

        @pl.when(odd)
        def _():
            over(step, 0).start()

    def whole(step, edge):
        @pl.when(even)
        def _():
            over(step, 0).wait_recv()
            if edge:
                across_edge(step, own).wait_recv()

        @pl.when(odd)
        def _():
            over(step, 1).wait_recv()

    def pass_on(step):
        across(step, own).wait_recv()
        hand_over(step)

    hand_over(0)
    for step in range(1, peers):
        across(step, peer(step, 1)).start()

    @pl.when(backward)
    def _():
        far(reach, even_place(0), time).wait_recv()

    @pl.when(even)
    def _():
        for step in range(1, peers):
            across_edge(step, peer(step, 1)).start()

    whole(0, False)

    for start in range(0, mine, TILE):
        x = window(store_ref, 0, pl.ds(start, TILE))
        middle, middle_sq = totals(x)
        for day in range(days):
            center, inverse = day_moments(x, middle, middle_sq, day)
            w = day_values(x, center, inverse * (1.0 / (WIN * shrink_level)), day)
            row_ref[day, :, start : start + TILE] = w
            high = w.astype(jnp.bfloat16).astype(jnp.float32)
            both = jnp.concatenate([high, w - high], 0)
            for sub in range(0, TILE, 128):
                turned = both[:, sub : sub + 128].T.astype(jnp.bfloat16)
                lhs_ref[day, start + sub : start + sub + 128, :128] = turned
                lhs_ref[day, start + sub : start + sub + 128, 128:] = turned

    per_block = mine // TILE
    pairs = per_block // 2
    strips = mine // STRIP
    block_steps = days * pairs * strips

    def prepare(block, parity, piece):
        tile, day = divmod(piece, days)
        cols = pl.ds(tile * TILE, TILE)
        if day == 0:
            x = window(store_ref, block, cols)
            x_ref[...] = x
            middle, middle_sq = totals(x)
            tot_ref[:8] = middle
            tot_ref[8:] = middle_sq
        x, middle, middle_sq = x_ref[...], tot_ref[:8], tot_ref[8:]
        s = store_ref[block, 0, :, cols].astype(jnp.float32)[day : day + 1]
        center, inverse = day_moments(x, middle, middle_sq, day)
        v = day_values(x, center, inverse * s, day)
        lin_ref[day] += v[:, :128] + v[:, 128:]
        high, low = halves(v)
        high_ref[parity, day, tile] = high
        low_ref[parity, day, tile] = low
        bound_ref[parity, day, tile] = jnp.broadcast_to(jnp.abs(s), (8, TILE))

    pieces = days * per_block

    def compute(*accs):
        def push(parity, place):
            day, pair = divmod(place, pairs)
            for unit in range(2):
                high = high_ref[parity, day, 2 * pair + unit]
                low = low_ref[parity, day, 2 * pair + unit]
                pltpu.matmul_push_rhs(
                    jnp.concatenate([high, high, low, low], 0),
                    staging_register=place % 2,
                    mxu_index=unit,
                )

        def take(parity, step):
            place, strip = divmod(step, strips)
            day, pair = divmod(place, pairs)
            rows = pl.ds(strip * STRIP, STRIP)
            part = None
            for unit in range(2):
                bound = bound_ref[parity, day, 2 * pair + unit][:1]
                got = pltpu.matmul_pop(accs[unit * strips + strip])
                kept = jnp.minimum(jnp.maximum(got, -bound), bound)
                kept = kept[:, :128] + kept[:, 128:]
                part = kept if part is None else part + kept
            sum_ref[day, rows, :] += part

        def steps(parity, first, last, piece_at=None, final=False, begin=False):
            for step in range(first, last):
                place, strip = divmod(step, strips)
                day = place // pairs
                lhs = lhs_ref[day, strip * STRIP : (strip + 1) * STRIP, :]
                for unit in range(2):
                    pltpu.matmul_acc_lhs(
                        accs[unit * strips + strip],
                        lhs,
                        load_staged_rhs=place % 2 if strip == 0 else None,
                    )
                if step >= LAG:
                    take(parity, step - LAG)
                elif not begin:
                    take(1 - parity, block_steps + step - LAG)
                if piece_at is not None:
                    piece_at(step)
                if strip == 0:
                    if step + strips < block_steps:
                        push(parity, place + 1)
                    elif not final:
                        push(1 - parity, 0)

        for piece in range(pieces):
            prepare(0, 0, piece)
        push(0, 0)
        quarter = block_steps // 4
        steps(0, 0, quarter, begin=True)
        pass_on(1)
        steps(0, quarter, 2 * quarter + quarter // 2)
        pass_on(2)
        steps(0, 2 * quarter + quarter // 2, 3 * quarter)
        whole(1, True)

        def first_pieces(step):
            for piece in range(pieces):
                if 3 * quarter + piece * (quarter // 2) // pieces == step:
                    prepare(1, 1, piece)

        steps(0, 3 * quarter, block_steps, first_pieces)

        def one_block(block, carry):
            parity = lax.rem(block, 2)
            whole(block + 1, True)

            def next_pieces(step):
                for piece in range(pieces):
                    if LAG + piece * (block_steps - strips - LAG) // pieces == step:
                        prepare(block + 1, 1 - parity, piece)

            steps(parity, 0, block_steps // 2, next_pieces)

            @pl.when(block + 2 < peers)
            def _():
                pass_on(block + 2)

            steps(parity, block_steps // 2, block_steps, next_pieces)
            return carry

        lax.fori_loop(1, peers - 1, one_block, 0)
        parity = (peers - 1) % 2
        steps(parity, 0, block_steps, final=True)
        for step in range(block_steps - LAG, block_steps):
            take(parity, step)

        for day in range(days):
            weight = jnp.sum(lin_ref[day], axis=1, keepdims=True)
            line = jnp.sum(row_ref[day] * weight, axis=0, keepdims=True)
            clamped = jnp.concatenate(
                [
                    jnp.sum(sum_ref[day, start : start + 128, :].T, axis=0, keepdims=True)
                    for start in range(0, mine, 128)
                ],
                1,
            )
            out_ref[day : day + 1, :] = (line - clamped) * shrink_level

    pl.run_scoped(
        compute,
        *[pltpu.ACC(unit)((STRIP, TILE), jnp.float32) for unit in range(2) for _ in range(strips)],
    )

    @pl.when(forward)
    def _():
        far(reach, even_place(0), time).wait_send()

    for back in range(2, reach, 2):
        @pl.when(time + back < times)
        def _(back=back):
            far(back, odd_place(reach - back), time).wait_send()

    for step in range(peers):
        if step:
            across(step, own).wait_send()

        @pl.when(even)
        def _(step=step):
            over(step, 1).wait_send()
            if step:
                across_edge(step, own).wait_send()

        @pl.when(odd)
        def _(step=step):
            over(step, 0).wait_send()


def per_device(returns, signal, earlier):
    days, mine = returns.shape
    peers = lax.axis_size("asset")
    tiles = mine // TILE
    place = pl.BlockSpec(memory_space=pl.ANY)
    vmem, dma = pltpu.VMEM, pltpu.SemaphoreType.DMA
    return pl.pallas_call(
        kernel,
        out_shape=jax.ShapeDtypeStruct((days, mine), jnp.float32),
        in_specs=[place] * 3,
        out_specs=pl.BlockSpec(memory_space=pltpu.VMEM),
        scratch_shapes=[
            vmem((peers, BLOCKS + 1, days, mine), jnp.bfloat16),
            vmem((BLOCKS - 1, days, mine), jnp.bfloat16),
            vmem((HIST, mine), jnp.bfloat16),
            vmem((2, days, tiles, DEPTH, TILE), jnp.bfloat16),
            vmem((2, days, tiles, DEPTH, TILE), jnp.bfloat16),
            vmem((2, days, tiles, 8, TILE), jnp.float32),
            vmem((days, mine, TILE), jnp.bfloat16),
            vmem((days, DEPTH, mine), jnp.float32),
            vmem((days, mine, 128), jnp.float32),
            vmem((days, DEPTH, 128), jnp.float32),
            vmem((DEPTH, TILE), jnp.float32),
            vmem((16, TILE), jnp.float32),
            dma((3,)),
        ]
        + [dma((BLOCKS // 2,))] * 2
        + [dma((peers,))] * 6,
        compiler_params=pltpu.CompilerParams(
            collective_id=0, has_side_effects=True, vmem_limit_bytes=48 << 20
        ),
        name="filter_days",
    )(returns, signal, earlier)


def solution(mesh):
    in_specs = (P("tm", "asset"), P("tm", "asset"), P(None, "asset"))
    out_specs = P("tm", "asset")
    return jax.shard_map(
        per_device, mesh=mesh, in_specs=in_specs, out_specs=out_specs, check_vma=False
    )
```

time: 165 us -> 45.7 us (0.28)
  the two profiles are of different devices: /device:TPU:16 before, /device:TPU:29 now
where the time goes in v3:
time: 45.7 us; the launch traced here: 45.5 us
  Pallas kernels  42.6 us (93%)
  local copies, waits for them, and re-layouts  2.9 us (6%)
    pallas_call x1, Pallas kernels, per_device(): pl.pallas_call(kernel, out_shape=jax.ShapeDtypeStruct((days, mine), jnp.f...  42.6 us
    unnamed x7, local copies, waits for them, and re-layouts  2.9 us

profile of v3, /device:TPU:29, one launch (start us, length us, event | category | flops | bytes accessed | tf_op | source)
XLA Modules:
  0.0 45.5 jit_solution(6883267179484428120)
XLA Ops:
  0.0 0.0 copy-start
  0.0 0.9 %copy-done = bf16[59,1024]{1,0:T(8,128)(2,1)S(1)} copy-done((bf16[59,1024]{1,0:T(8,128)(2,1)S(1)}, bf16[59,1024]{1,0:T(8,128)(2,1)}, u32[]{:S(2)}) %copy-start) | copy-done | bytes 120856
  0.9 0.0 copy-start.1
  0.9 0.7 %copy-done.1 = bf16[4,1024]{1,0:T(4,128)(2,1)S(1)} copy-done((bf16[4,1024]{1,0:T(4,128)(2,1)S(1)}, bf16[4,1024]{1,0:T(4,128)(2,1)}, u32[]{:S(2)}) %copy-start.1) | copy-done | bytes 8216
  1.6 0.0 copy-start.2
  1.6 0.7 %copy-done.2 = bf16[4,1024]{1,0:T(4,128)(2,1)S(1)} copy-done((bf16[4,1024]{1,0:T(4,128)(2,1)S(1)}, bf16[4,1024]{1,0:T(4,128)(2,1)}, u32[]{:S(2)}) %copy-start.2) | copy-done | bytes 8216
  2.3 42.6 %filter_days.1 = f32[4,1024]{1,0:T(4,128)S(1)} custom-call(bf16[4,1024]{1,0:T(4,128)(2,1)S(1)} %copy-done.1, bf16[4,1024]{1,0:T(4,128)(2,1)S(1)} %copy-done.2, bf16[59,1024]{1,0:T(8,128)(2,1)S(1)} %copy-done), custom_call_target="tpu_custom_call" | custom-call | tf_op jit(solution)/shard_map/filter_days/pallas_call | solution.py:412
  44.9 0.6 %copy.5 = f32[4,1024]{1,0:T(4,128)} copy(f32[4,1024]{1,0:T(4,128)S(1)} %filter_days.1) | data formatting | bytes 32768
Async XLA Ops:
  0.0 0.9 %copy-start = (bf16[59,1024]{1,0:T(8,128)(2,1)S(1)}, bf16[59,1024]{1,0:T(8,128)(2,1)}, u32[]{:S(2)}) copy-start(bf16[59,1024]{1,0:T(8,128)(2,1)} %earlier_ref.1) | copy-start | bytes 362500
  0.9 0.7 %copy-start.1 = (bf16[4,1024]{1,0:T(4,128)(2,1)S(1)}, bf16[4,1024]{1,0:T(4,128)(2,1)}, u32[]{:S(2)}) copy-start(bf16[4,1024]{1,0:T(4,128)(2,1)} %returns_ref.1) | copy-start | bytes 24580
  1.6 0.7 %copy-start.2 = (bf16[4,1024]{1,0:T(4,128)(2,1)S(1)}, bf16[4,1024]{1,0:T(4,128)(2,1)}, u32[]{:S(2)}) copy-start(bf16[4,1024]{1,0:T(4,128)(2,1)} %signal_ref.1) | copy-start | bytes 24580

commit v4 on v3

--- a/solution.py
+++ b/solution.py
@@ -218,17 +218,22 @@
         hand_over(step)
 
     hand_over(0)
-    for step in range(1, peers):
-        across(step, peer(step, 1)).start()
+    def send_window(first, last):
+        for step in range(first, last):
+            across(step, peer(step, 1)).start()
+
+        @pl.when(even)
+        def _():
+            for step in range(first, last):
+                across_edge(step, peer(step, 1)).start()
+
+    nearest = peers // 2
 
     @pl.when(backward)
     def _():
         far(reach, even_place(0), time).wait_recv()
 
-    @pl.when(even)
-    def _():
-        for step in range(1, peers):
-            across_edge(step, peer(step, 1)).start()
+    send_window(1, nearest)
 
     whole(0, False)
 
@@ -326,6 +331,7 @@
         quarter = block_steps // 4
         steps(0, 0, quarter, begin=True)
         pass_on(1)
+        send_window(nearest, peers)
         steps(0, quarter, 2 * quarter + quarter // 2)
         pass_on(2)
         steps(0, 2 * quarter + quarter // 2, 3 * quarter)
@@ -435,7 +441,7 @@
             collective_id=0, has_side_effects=True, vmem_limit_bytes=48 << 20
         ),
         name="filter_days",
-    )(returns, signal, earlier)
+    )(*(pltpu.with_memory_space_constraint(x, pltpu.HBM) for x in (returns, signal, earlier)))
 
 
 def solution(mesh):

time: 45.7 us -> 39.3 us (0.86)
  the two profiles are of different devices: /device:TPU:29 before, /device:TPU:16 now
where the time goes in v4:
time: 39.3 us; the launch traced here: 39.1 us
  Pallas kernels  38.4 us (98%)
  local copies, waits for them, and re-layouts  0.61 us (2%)
    pallas_call x1, Pallas kernels, per_device(): pl.pallas_call(kernel, out_shape=jax.ShapeDtypeStruct((days, mine), jnp.f...  38.4 us

profile of v4, /device:TPU:16, one launch (start us, length us, event | category | flops | bytes accessed | tf_op | source)
XLA Modules:
  0.0 39.1 jit_solution(7665016373163180787)
XLA Ops:
  0.0 38.4 %filter_days.1 = f32[4,1024]{1,0:T(4,128)S(1)} custom-call(bf16[4,1024]{1,0:T(4,128)(2,1)} %returns_ref.1, bf16[4,1024]{1,0:T(4,128)(2,1)} %signal_ref.1, bf16[59,1024]{1,0:T(8,128)(2,1)} %earlier_ref.1), custom_call_target="tpu_custom_call" | custom-call | tf_op jit(solution)/shard_map/filter_days/pallas_call | solution.py:418
  38.5 0.6 %copy.5 = f32[4,1024]{1,0:T(4,128)} copy(f32[4,1024]{1,0:T(4,128)S(1)} %filter_days.1) | data formatting | bytes 32768

commit v5 on v4

--- a/solution.py
+++ b/solution.py
@@ -10,7 +10,8 @@
 DEPTH = 64
 TILE = 256
 STRIP = 128
-LAG = 4
+LAG = 0
+SPARE = 8
 BLOCKS = 16
 
 var_floor = 0.05
@@ -65,7 +66,7 @@
 
 
 def window(store_ref, block, cols):
-    x = store_ref[block, 1:, :, cols].astype(jnp.float32)
+    x = store_ref[block, 1 : 1 + BLOCKS, :, cols].astype(jnp.float32)
     return x.reshape(DEPTH, TILE)
 
 
@@ -176,56 +177,36 @@
 
     def across_edge(step, to):
         return pltpu.make_async_remote_copy(
-            src_ref=store_ref.at[0, even_place(0)],
-            dst_ref=store_ref.at[step, even_place(0)],
+            src_ref=store_ref.at[0, even_place(0) - core],
+            dst_ref=store_ref.at[step, even_place(0) + core * SPARE],
             send_sem=send_edge.at[step],
             recv_sem=got_edge.at[step],
             **at(time, to),
         )
 
-    def over(step, low):
-        size = 7 + low
+    def over(step):
         return pltpu.make_async_remote_copy(
-            src_ref=store_ref.at[step, pl.ds(1, size)],
-            dst_ref=store_ref.at[step, pl.ds(10 - low, size)],
+            src_ref=store_ref.at[step, pl.ds(1, 8)],
+            dst_ref=store_ref.at[step, pl.ds(9 + core, 8)],
             send_sem=send_twin.at[step],
             recv_sem=got_twin.at[step],
             **at(twin, own),
         )
 
-    def hand_over(step):
-        @pl.when(even)
-        def _():
-            over(step, 1).start()
-
-        @pl.when(odd)
-        def _():
-            over(step, 0).start()
-
     def whole(step, edge):
-        @pl.when(even)
-        def _():
-            over(step, 0).wait_recv()
-            if edge:
-                across_edge(step, own).wait_recv()
-
-        @pl.when(odd)
-        def _():
-            over(step, 1).wait_recv()
+        over(step).wait_recv()
+        if edge:
+            across_edge(step, own).wait_recv()
 
     def pass_on(step):
         across(step, own).wait_recv()
-        hand_over(step)
-
-    hand_over(0)
+        over(step).start()
+
+    over(0).start()
     def send_window(first, last):
         for step in range(first, last):
             across(step, peer(step, 1)).start()
-
-        @pl.when(even)
-        def _():
-            for step in range(first, last):
-                across_edge(step, peer(step, 1)).start()
+            across_edge(step, peer(step, 1)).start()
 
     nearest = peers // 2
 
@@ -236,27 +217,13 @@
     send_window(1, nearest)
 
     whole(0, False)
-
-    for start in range(0, mine, TILE):
-        x = window(store_ref, 0, pl.ds(start, TILE))
-        middle, middle_sq = totals(x)
-        for day in range(days):
-            center, inverse = day_moments(x, middle, middle_sq, day)
-            w = day_values(x, center, inverse * (1.0 / (WIN * shrink_level)), day)
-            row_ref[day, :, start : start + TILE] = w
-            high = w.astype(jnp.bfloat16).astype(jnp.float32)
-            both = jnp.concatenate([high, w - high], 0)
-            for sub in range(0, TILE, 128):
-                turned = both[:, sub : sub + 128].T.astype(jnp.bfloat16)
-                lhs_ref[day, start + sub : start + sub + 128, :128] = turned
-                lhs_ref[day, start + sub : start + sub + 128, 128:] = turned
 
     per_block = mine // TILE
     pairs = per_block // 2
     strips = mine // STRIP
     block_steps = days * pairs * strips
 
-    def prepare(block, parity, piece):
+    def prepare(block, parity, piece, both_sides=False):
         tile, day = divmod(piece, days)
         cols = pl.ds(tile * TILE, TILE)
         if day == 0:
@@ -274,6 +241,16 @@
         high_ref[parity, day, tile] = high
         low_ref[parity, day, tile] = low
         bound_ref[parity, day, tile] = jnp.broadcast_to(jnp.abs(s), (8, TILE))
+        if both_sides:
+            start = tile * TILE
+            w = day_values(x, center, inverse * (1.0 / (WIN * shrink_level)), day)
+            row_ref[day, :, start : start + TILE] = w
+            high = w.astype(jnp.bfloat16).astype(jnp.float32)
+            both = jnp.concatenate([high, w - high], 0)
+            for sub in range(0, TILE, 128):
+                turned = both[:, sub : sub + 128].T.astype(jnp.bfloat16)
+                lhs_ref[day, start + sub : start + sub + 128, :128] = turned
+                lhs_ref[day, start + sub : start + sub + 128, 128:] = turned
 
     pieces = days * per_block
 
@@ -326,15 +303,14 @@
                         push(1 - parity, 0)
 
         for piece in range(pieces):
-            prepare(0, 0, piece)
+            prepare(0, 0, piece, True)
         push(0, 0)
         quarter = block_steps // 4
-        steps(0, 0, quarter, begin=True)
+        steps(0, 0, quarter + 4, begin=True)
         pass_on(1)
         send_window(nearest, peers)
-        steps(0, quarter, 2 * quarter + quarter // 2)
+        steps(0, quarter + 4, 3 * quarter)
         pass_on(2)
-        steps(0, 2 * quarter + quarter // 2, 3 * quarter)
         whole(1, True)
 
         def first_pieces(step):
@@ -348,18 +324,16 @@
             parity = lax.rem(block, 2)
             whole(block + 1, True)
 
-            def next_pieces(step):
-                for piece in range(pieces):
-                    if LAG + piece * (block_steps - strips - LAG) // pieces == step:
-                        prepare(block + 1, 1 - parity, piece)
-
-            steps(parity, 0, block_steps // 2, next_pieces)
-
             @pl.when(block + 2 < peers)
             def _():
                 pass_on(block + 2)
 
-            steps(parity, block_steps // 2, block_steps, next_pieces)
+            def next_pieces(step):
+                for piece in range(pieces):
+                    if 4 + piece * (block_steps - strips - 4) // pieces == step:
+                        prepare(block + 1, 1 - parity, piece)
+
+            steps(parity, 0, block_steps, next_pieces)
             return carry
 
         lax.fori_loop(1, peers - 1, one_block, 0)
@@ -395,18 +369,10 @@
             far(back, odd_place(reach - back), time).wait_send()
 
     for step in range(peers):
+        over(step).wait_send()
         if step:
             across(step, own).wait_send()
-
-        @pl.when(even)
-        def _(step=step):
-            over(step, 1).wait_send()
-            if step:
-                across_edge(step, own).wait_send()
-
-        @pl.when(odd)
-        def _(step=step):
-            over(step, 0).wait_send()
+            across_edge(step, own).wait_send()
 
 
 def per_device(returns, signal, earlier):
@@ -421,7 +387,7 @@
         in_specs=[place] * 3,
         out_specs=pl.BlockSpec(memory_space=pltpu.VMEM),
         scratch_shapes=[
-            vmem((peers, BLOCKS + 1, days, mine), jnp.bfloat16),
+            vmem((peers, BLOCKS + 2, days, mine), jnp.bfloat16),
             vmem((BLOCKS - 1, days, mine), jnp.bfloat16),
             vmem((HIST, mine), jnp.bfloat16),
             vmem((2, days, tiles, DEPTH, TILE), jnp.bfloat16),

time: 39.3 us -> 38.2 us (0.972)
  Pallas kernels: 38.4 us -> 37.4 us
    pallas_call x1, Pallas kernels: 38.4 us -> 37.4 us  [per_device(): pl.pallas_call(kernel, out_shape=jax.ShapeDtypeStruct((days, mine), jnp.f...]
where the time goes in v5:
time: 38.2 us; the launch traced here: 38.1 us
  Pallas kernels  37.4 us (98%)
  local copies, waits for them, and re-layouts  0.61 us (2%)
    pallas_call x1, Pallas kernels, per_device(): pl.pallas_call(kernel, out_shape=jax.ShapeDtypeStruct((days, mine), jnp.f...  37.4 us

profile of v5, /device:TPU:16, one launch (start us, length us, event | category | flops | bytes accessed | tf_op | source)
XLA Modules:
  0.0 38.1 jit_solution(4613497856340360915)
XLA Ops:
  0.0 37.4 %filter_days.1 = f32[4,1024]{1,0:T(4,128)S(1)} custom-call(bf16[4,1024]{1,0:T(4,128)(2,1)} %returns_ref.1, bf16[4,1024]{1,0:T(4,128)(2,1)} %signal_ref.1, bf16[59,1024]{1,0:T(8,128)(2,1)} %earlier_ref.1), custom_call_target="tpu_custom_call" | custom-call | tf_op jit(solution)/shard_map/filter_days/pallas_call | solution.py:384
  37.4 0.6 %copy.5 = f32[4,1024]{1,0:T(4,128)} copy(f32[4,1024]{1,0:T(4,128)S(1)} %filter_days.1) | data formatting | bytes 32768

commit v6 on v5

--- a/solution.py
+++ b/solution.py
@@ -12,6 +12,11 @@
 STRIP = 128
 LAG = 0
 SPARE = 8
+FIRST_WAIT = 28
+SECOND_WAIT = 52
+OWN_AT = (0, 4, 8, 12)
+PIECE_AT = 4
+PIECE_SPAN = 60
 BLOCKS = 16
 
 var_floor = 0.05
@@ -228,11 +233,11 @@
         cols = pl.ds(tile * TILE, TILE)
         if day == 0:
             x = window(store_ref, block, cols)
-            x_ref[...] = x
+            x_ref[tile] = x
             middle, middle_sq = totals(x)
-            tot_ref[:8] = middle
-            tot_ref[8:] = middle_sq
-        x, middle, middle_sq = x_ref[...], tot_ref[:8], tot_ref[8:]
+            tot_ref[tile, :8] = middle
+            tot_ref[tile, 8:] = middle_sq
+        x, middle, middle_sq = x_ref[tile], tot_ref[tile, :8], tot_ref[tile, 8:]
         s = store_ref[block, 0, :, cols].astype(jnp.float32)[day : day + 1]
         center, inverse = day_moments(x, middle, middle_sq, day)
         v = day_values(x, center, inverse * s, day)
@@ -302,23 +307,30 @@
                     elif not final:
                         push(1 - parity, 0)
 
-        for piece in range(pieces):
-            prepare(0, 0, piece, True)
+        quarter = block_steps // 4
+        for tile in range(per_block):
+            prepare(0, 0, tile * days, True)
+
+        def own_pieces(step):
+            day, within = divmod(step, quarter)
+            for tile in range(per_block):
+                if day + 1 < days and within == OWN_AT[tile]:
+                    prepare(0, 0, tile * days + day + 1, True)
+
         push(0, 0)
-        quarter = block_steps // 4
-        steps(0, 0, quarter + 4, begin=True)
+        steps(0, 0, FIRST_WAIT, own_pieces, begin=True)
         pass_on(1)
         send_window(nearest, peers)
-        steps(0, quarter + 4, 3 * quarter)
+        steps(0, FIRST_WAIT, SECOND_WAIT, own_pieces)
         pass_on(2)
         whole(1, True)
 
         def first_pieces(step):
             for piece in range(pieces):
-                if 3 * quarter + piece * (quarter // 2) // pieces == step:
+                if SECOND_WAIT + piece * (block_steps - SECOND_WAIT - 1) // pieces == step:
                     prepare(1, 1, piece)
 
-        steps(0, 3 * quarter, block_steps, first_pieces)
+        steps(0, SECOND_WAIT, block_steps, first_pieces)
 
         def one_block(block, carry):
             parity = lax.rem(block, 2)
@@ -330,7 +342,7 @@
 
             def next_pieces(step):
                 for piece in range(pieces):
-                    if 4 + piece * (block_steps - strips - 4) // pieces == step:
+                    if PIECE_AT + piece * PIECE_SPAN // pieces == step:
                         prepare(block + 1, 1 - parity, piece)
 
             steps(parity, 0, block_steps, next_pieces)
@@ -397,8 +409,8 @@
             vmem((days, DEPTH, mine), jnp.float32),
             vmem((days, mine, 128), jnp.float32),
             vmem((days, DEPTH, 128), jnp.float32),
-            vmem((DEPTH, TILE), jnp.float32),
-            vmem((16, TILE), jnp.float32),
+            vmem((tiles, DEPTH, TILE), jnp.float32),
+            vmem((tiles, 16, TILE), jnp.float32),
             dma((3,)),
         ]
         + [dma((BLOCKS // 2,))] * 2

time: 38.2 us -> 38.1 us (level)
  no operation moved by 1% of the time
where the time goes in v6:
time: 38.1 us; the launch traced here: 37.9 us
  Pallas kernels  37.3 us (98%)
  local copies, waits for them, and re-layouts  0.61 us (2%)
    pallas_call x1, Pallas kernels, per_device(): pl.pallas_call(kernel, out_shape=jax.ShapeDtypeStruct((days, mine), jnp.f...  37.3 us

profile of v6, /device:TPU:16, one launch (start us, length us, event | category | flops | bytes accessed | tf_op | source)
XLA Modules:
  0.0 37.9 jit_solution(8425846157560675911)
XLA Ops:
  0.0 37.3 %filter_days.1 = f32[4,1024]{1,0:T(4,128)S(1)} custom-call(bf16[4,1024]{1,0:T(4,128)(2,1)} %returns_ref.1, bf16[4,1024]{1,0:T(4,128)(2,1)} %signal_ref.1, bf16[59,1024]{1,0:T(8,128)(2,1)} %earlier_ref.1), custom_call_target="tpu_custom_call" | custom-call | tf_op jit(solution)/shard_map/filter_days/pallas_call | solution.py:396
  37.3 0.6 %copy.5 = f32[4,1024]{1,0:T(4,128)} copy(f32[4,1024]{1,0:T(4,128)S(1)} %filter_days.1) | data formatting | bytes 32768

commit v7 on v6

--- a/solution.py
+++ b/solution.py
@@ -170,19 +170,19 @@
         def _(back=back):
             far(back, odd_place(reach - back), time).wait_recv()
 
-    def across(step, to):
+    def across(step, to, held=0):
         half = pl.ds(0, 9)
         return pltpu.make_async_remote_copy(
-            src_ref=store_ref.at[0, half],
+            src_ref=store_ref.at[held, half],
             dst_ref=store_ref.at[step, half],
             send_sem=send_peer.at[step],
             recv_sem=got_peer.at[step],
             **at(time, to),
         )
 
-    def across_edge(step, to):
+    def across_edge(step, to, held=0):
         return pltpu.make_async_remote_copy(
-            src_ref=store_ref.at[0, even_place(0) - core],
+            src_ref=store_ref.at[held, even_place(0) - core],
             dst_ref=store_ref.at[step, even_place(0) + core * SPARE],
             send_sem=send_edge.at[step],
             recv_sem=got_edge.at[step],
@@ -208,18 +208,22 @@
         over(step).start()
 
     over(0).start()
-    def send_window(first, last):
-        for step in range(first, last):
-            across(step, peer(step, 1)).start()
-            across_edge(step, peer(step, 1)).start()
-
-    nearest = peers // 2
+    nearest, opposite, relayed = peers // 2, peers // 2, peers - 1
+
+    for step in range(1, nearest):
+        across(step, peer(step, 1)).start()
 
     @pl.when(backward)
     def _():
         far(reach, even_place(0), time).wait_recv()
 
-    send_window(1, nearest)
+    for step in range(1, nearest):
+        across_edge(step, peer(step, 1)).start()
+
+    def send_rest():
+        for step in range(nearest, relayed):
+            across(step, peer(step, 1)).start()
+            across_edge(step, peer(step, 1)).start()
 
     whole(0, False)
 
@@ -320,7 +324,7 @@
         push(0, 0)
         steps(0, 0, FIRST_WAIT, own_pieces, begin=True)
         pass_on(1)
-        send_window(nearest, peers)
+        send_rest()
         steps(0, FIRST_WAIT, SECOND_WAIT, own_pieces)
         pass_on(2)
         whole(1, True)
@@ -339,6 +343,14 @@
             @pl.when(block + 2 < peers)
             def _():
                 pass_on(block + 2)
+
+            @pl.when(block + 2 == opposite)
+            def _():
+                across(relayed, peer(1, 1), opposite).start()
+
+            @pl.when(block + 1 == opposite)
+            def _():
+                across_edge(relayed, peer(1, 1), opposite).start()
 
             def next_pieces(step):
                 for piece in range(pieces):

time: 38.1 us -> 37.8 us (level)
  no operation moved by 1% of the time
where the time goes in v7:
time: 37.8 us; the launch traced here: 37.6 us
  Pallas kernels  37 us (98%)
  local copies, waits for them, and re-layouts  0.61 us (2%)
    pallas_call x1, Pallas kernels, per_device(): pl.pallas_call(kernel, out_shape=jax.ShapeDtypeStruct((days, mine), jnp.f...  37 us

profile of v7, /device:TPU:16, one launch (start us, length us, event | category | flops | bytes accessed | tf_op | source)
XLA Modules:
  0.0 37.6 jit_solution(1990759836428449538)
XLA Ops:
  0.0 37.0 %filter_days.1 = f32[4,1024]{1,0:T(4,128)S(1)} custom-call(bf16[4,1024]{1,0:T(4,128)(2,1)} %returns_ref.1, bf16[4,1024]{1,0:T(4,128)(2,1)} %signal_ref.1, bf16[59,1024]{1,0:T(8,128)(2,1)} %earlier_ref.1), custom_call_target="tpu_custom_call" | custom-call | tf_op jit(solution)/shard_map/filter_days/pallas_call | solution.py:408
  37.0 0.6 %copy.5 = f32[4,1024]{1,0:T(4,128)} copy(f32[4,1024]{1,0:T(4,128)S(1)} %filter_days.1) | data formatting | bytes 32768

commit v8 on v7

--- a/solution.py
+++ b/solution.py
@@ -324,9 +324,9 @@
         push(0, 0)
         steps(0, 0, FIRST_WAIT, own_pieces, begin=True)
         pass_on(1)
+        pass_on(2)
         send_rest()
         steps(0, FIRST_WAIT, SECOND_WAIT, own_pieces)
-        pass_on(2)
         whole(1, True)
 
         def first_pieces(step):

time: 37.8 us -> 38.1 us (level)
  Pallas kernels: 37 us -> 37.4 us
where the time goes in v8:
time: 38.1 us; the launch traced here: 38 us
  Pallas kernels  37.4 us (98%)
  local copies, waits for them, and re-layouts  0.61 us (2%)
    pallas_call x1, Pallas kernels, per_device(): pl.pallas_call(kernel, out_shape=jax.ShapeDtypeStruct((days, mine), jnp.f...  37.4 us

profile of v8, /device:TPU:16, one launch (start us, length us, event | category | flops | bytes accessed | tf_op | source)
XLA Modules:
  0.0 38.0 jit_solution(749675991099154903)
XLA Ops:
  0.0 37.4 %filter_days.1 = f32[4,1024]{1,0:T(4,128)S(1)} custom-call(bf16[4,1024]{1,0:T(4,128)(2,1)} %returns_ref.1, bf16[4,1024]{1,0:T(4,128)(2,1)} %signal_ref.1, bf16[59,1024]{1,0:T(8,128)(2,1)} %earlier_ref.1), custom_call_target="tpu_custom_call" | custom-call | tf_op jit(solution)/shard_map/filter_days/pallas_call | solution.py:408
  37.4 0.6 %copy.5 = f32[4,1024]{1,0:T(4,128)} copy(f32[4,1024]{1,0:T(4,128)S(1)} %filter_days.1) | data formatting | bytes 32768
